TPU v7x, 128 devices: a whole 4x4x4 slice. The times are simulated.
128 devices in a mesh: eq: 8 (over x, z_hi), row: 4 (over y), col: 4 (over z_lo, core).
Axes of the slice: x: 4, y: 4, z: 4 (z_hi: 2, z_lo: 2; z = z_hi * 2 + z_lo), core: 2. Of those that a mesh axis runs over, the one named last changes fastest.
Arguments:
- transition: float32 [24576, 3072], P(('eq', 'row'), 'col'), parts along dimension 0, may hold values from -0.05 to 0.9
- covariance: float32 [24576, 3072], P(('eq', 'row'), 'col'), parts along dimension 0, may hold values from -1 to 5, as said below
Outputs:
- covariance_out: float32 [24576, 3072], P(('eq', 'row'), 'col'), parts along dimension 0
- transition_out: float32 [24576, 3072], P(('eq', 'row'), 'col'), parts along dimension 0
There are 8 independent parts, one for each index of `eq`. A program takes and returns all parts, laid end to end along the dimension named above; each array names one. Nothing has to cross between parts.
Inputs may be any that keep to these rules, and one draw needn't show every extreme that they name: covariance is exactly symmetric.
All inputs are finite; a program needn't handle non-finite values.
Results may differ from a plain program's by a relative error of at most 0.0001.
Values sent between devices are 32-bit elements; how exact they have to be, the bound alone decides.
A program may use at most 128 MiB of HBM per device.

v0:
```python
import jax
import jax.numpy as jnp
from jax import lax

STEPS = 1


def reference(transition, covariance):
    highest = lax.Precision.HIGHEST
    matrix = transition
    current = covariance
    for repeat in range(STEPS):
        product = jnp.dot(matrix, current, precision=highest, preferred_element_type=jnp.float32)
        current = (
            jnp.dot(product, matrix.T, precision=highest, preferred_element_type=jnp.float32)
            + current
        )
        matrix = jnp.dot(matrix, matrix, precision=highest, preferred_element_type=jnp.float32)
    return (current, matrix)


def apart(x, dim, parts):
    return x.reshape(x.shape[:dim] + (parts, x.shape[dim] // parts) + x.shape[dim + 1 :])


def together(x, dim):
    return x.reshape(x.shape[:dim] + (x.shape[dim] * x.shape[dim + 1],) + x.shape[dim + 2 :])


def solution(mesh):
    parts = mesh.shape["eq"]

    def whole(*arrays):
        each = [a if d is None else apart(a, d, parts) for a, d in zip(arrays, (0, 0))]
        made = jax.vmap(reference, in_axes=(0, 0), out_axes=(0, 0))(*each)
        return tuple(together(a, d) for a, d in zip(made, (0, 0)))

    return whole
```

profile of v0, /device:TPU:1, one launch (start us, length us, event | category | flops | bytes accessed | tf_op | source)
XLA Modules:
  0.0 417.8 jit_solution(8428018006764190129)
XLA Ops:
  7.2 0.0 all-gather.18.cloned.1.call-start
  7.2 0.7 all-gather.18.cloned.1.call-update
  7.9 0.0 all-gather.20.cloned.1.call-start
  7.9 0.7 all-gather.20.cloned.1.call-update
  8.6 0.0 all-gather.22.cloned.1.call-start
  8.7 0.7 all-gather.22.cloned.1.call-update
  9.4 0.0 reduce-scatter.4.cloned.1.call-start
  9.4 94.0 %all-gather.18.cloned.1.call-done = f32[768,3072]{1,0:T(8,128)} async-done(((f32[768,768]{1,0:T(8,128)}), f32[768,3072]{1,0:T(8,128)}) %all-gather.18.cloned.1.call-update) | async-done | bytes 9437200 | tf_op jit(solution)/reshape | solution.py:23
  103.4 93.9 %all-gather.20.cloned.1.call-done = f32[3072,768]{1,0:T(8,128)} async-done(((f32[768,768]{1,0:T(8,128)}), f32[3072,768]{1,0:T(8,128)}) %all-gather.20.cloned.1.call-update) | async-done | bytes 9437200 | tf_op jit(solution)/reshape | solution.py:23
  197.3 26.0 %fusion.1 = f32[768,768]{1,0:T(8,128)S(1)} fusion(f32[768,3072]{1,0:T(8,128)} %all-gather.18.cloned.1.call-done, f32[3072,768]{1,0:T(8,128)} %all-gather.20.cloned.1.call-done), kind=kOutput, calls=%fused_computation.3 | convolution fusion | flops 21743271936 | bytes 21233664 | tf_op jit(solution)/vmap()/dot_general | solution.py:13
  223.4 68.5 %all-gather.22.cloned.1.call-done = f32[3072,768]{1,0:T(8,128)} async-done(((f32[768,768]{1,0:T(8,128)}), f32[3072,768]{1,0:T(8,128)}) %all-gather.22.cloned.1.call-update) | async-done | bytes 9437200 | tf_op jit(solution)/reshape | solution.py:23
  291.9 26.8 %convolution_bitcast_fusion = f32[1,768,3072]{2,1,0:T(8,128)} fusion(f32[768,768]{1,0:T(8,128)S(1)} %fusion.1, f32[3072,768]{1,0:T(8,128)} %all-gather.22.cloned.1.call-done), kind=kOutput, calls=%fused_computation | convolution fusion | flops 21743271936 | bytes 21233664 | tf_op jit(solution)/vmap()/dot_general | solution.py:15
  318.7 0.0 reduce-scatter.4.cloned.1.call-update
  318.8 0.0 copy-start
  318.8 27.7 %fusion.2 = f32[768,768]{1,0:T(8,128)} fusion(f32[768,3072]{1,0:T(8,128)} %all-gather.18.cloned.1.call-done, f32[3072,768]{1,0:T(8,128)} %all-gather.22.cloned.1.call-done), kind=kOutput, calls=%fused_computation.4 | convolution fusion | flops 21743271936 | bytes 21233664 | tf_op jit(solution)/vmap()/dot_general | solution.py:18
  346.5 61.4 %reduce-scatter.4.cloned.1.call-done = f32[1,768,768]{2,1,0:T(8,128)} async-done(((f32[1,768,3072]{2,1,0:T(8,128)}), f32[1,768,768]{2,1,0:T(8,128)}) %reduce-scatter.4.cloned.1.call-update) | async-done | bytes 2359312
  407.9 0.0 copy-done
  407.9 3.4 fusion
Async XLA Ops:
  7.2 96.3 %all-gather.18.cloned.1.call-start = ((), (), s32[]{:S(2)}) async-start(), calls=%async_computation.1 | async-start | bytes 11796480 | tf_op jit(solution)/reshape | solution.py:23
  7.9 189.4 %all-gather.20.cloned.1.call-start = ((), (), s32[]{:S(2)}) async-start(), calls=%async_computation.2 | async-start | bytes 11796480 | tf_op jit(solution)/reshape | solution.py:23
  8.6 283.3 %all-gather.22.cloned.1.call-start = ((), (), s32[]{:S(2)}) async-start(), calls=%async_computation.3 | async-start | bytes 11796480 | tf_op jit(solution)/reshape | solution.py:23
  9.4 398.5 %reduce-scatter.4.cloned.1.call-start = ((), (), s32[]{:S(2)}) async-start(), calls=%async_computation.4 | async-start | bytes 11796480
  318.8 89.1 %copy-start = (f32[768,768]{1,0:T(8,128)S(1)}, f32[768,768]{1,0:T(8,128)}, u32[]{:S(2)}) copy-start(f32[768,768]{1,0:T(8,128)} %param.1) | copy-start | bytes 7077892
Sparse Core Ops, SparseCore 0:
  9.6 93.7 all-gather.17
  105.1 92.1 all-gather.19
  199.0 92.8 all-gather.21
  318.9 88.9 reduce-scatter.3
where the time goes:
time: 418 us
  waiting for transfers between devices  320 us (77%)
  matrix products  80.6 us (19%)
  between operations  13.8 us (3%)
    reshape x3, waiting for transfers between devices, apart(): x.reshape(x.shape[:dim] + (parts, x.shape[dim] // parts) + x.shape[dim +...  256 us
    unnamed x5, waiting for transfers between devices  63.4 us
    dot_general x1, matrix products, reference(): jnp.dot(matrix, matrix, precision=highest, preferred_element_type=jnp.flo...  27.7 us
    dot_general x1, matrix products, reference(): jnp.dot(product, matrix.T, precision=highest, preferred_element_type=jnp....  26.8 us
    dot_general x1, matrix products, reference(): jnp.dot(matrix, current, precision=highest, preferred_element_type=jnp.fl...  26 us
  transfers between devices with their start and end apart: 4, of which 4 were waited for; matrix products, arithmetic and copies ran while one was open for 13% of the time, Pallas kernels for 0%

commit v1 on v0

v1 whole, which is shorter than its diff:
```python
import jax
import jax.numpy as jnp
from jax import lax
from jax.experimental import pallas as pl
from jax.experimental.pallas import tpu as pltpu
from jax.sharding import PartitionSpec as P

N = 768
G = 256
NG = N // G
H = G // 2
BF = jnp.bfloat16
F32 = jnp.float32


def split(x):
    hi = x.astype(BF)
    lo = (x - hi.astype(F32)).astype(BF)
    return hi, lo


def dot(a, b, contract):
    return lax.dot_general(a, b, (contract, ((), ())), preferred_element_type=F32)


def dot3(ah, al, bh, bl, contract):
    return dot(ah, bh, contract) + (dot(ah, bl, contract) + dot(al, bh, contract))


NN = ((1,), (0,))
NT = ((1,), (1,))


def kernel(
    a_hbm,
    x_hbm,
    xo,
    a2,
    xcol,
    acol,
    arow,
    arh,
    arl,
    yh,
    yl,
    ch,
    cl,
    psend,
    precv,
    pkeep,
    pzrecv,
    lsem,
    rs,
    rr,
    ws,
    wr,
    ps,
    pr,
    zs,
    zr,
):
    y = lax.axis_index("row")
    c = lax.axis_index("col")
    right, left = (y + 1) % 4, (y + 3) % 4
    partner = c + 1 - 2 * (c % 2)
    other = (c + 2) % 4
    other_partner = (partner + 2) % 4

    load_a = pltpu.make_async_copy(a_hbm, acol.at[0], lsem.at[0])
    load_x = pltpu.make_async_copy(x_hbm, xcol.at[0], lsem.at[1])
    load_x.start()
    load_a.start()

    barrier = pltpu.get_barrier_semaphore()
    for where in ({"row": left}, {"row": right}, {"col": partner}, {"col": other}):
        pl.semaphore_signal(barrier, inc=1, device_id=where, device_id_type=pl.DeviceIdType.MESH)
    pl.semaphore_wait(barrier, 4)

    def remote(src, dst, send, recv, where):
        return pltpu.make_async_remote_copy(
            src_ref=src,
            dst_ref=dst,
            send_sem=send,
            recv_sem=recv,
            device_id=where,
            device_id_type=pl.DeviceIdType.MESH,
        )

    cols = (xcol, acol)

    def near(arr, d, g):
        ref = cols[arr]
        rows = pl.ds(g * G, G)
        return remote(
            ref.at[0, rows],
            ref.at[1 + d, rows],
            rs.at[arr, d, 0, g],
            rr.at[arr, d, 0, g],
            {"row": right if d == 0 else left},
        )

    def far(arr, d, g):
        ref = cols[arr]
        rows = pl.ds(g * G + d * H, H)
        return remote(
            ref.at[1 + d, rows],
            ref.at[3, rows],
            rs.at[arr, d, 1, g],
            rr.at[arr, d, 1, g],
            {"row": right if d == 0 else left},
        )

    def both(make, arr, g):
        return [make(arr, d, g) for d in range(2)]

    def start(copies):
        for copy in copies:
            copy.start()

    def arrived(copies):
        for copy in copies:
            copy.wait_recv()

    row_partner = remote(acol.at[0], arow.at[0], ws.at[0], wr.at[0], {"col": partner})

    def row_other(g):
        rows = pl.ds(g * G, G)
        return remote(acol.at[0, rows], arow.at[1, rows], ws.at[1 + g], wr.at[1 + g], {"col": other})

    def row_forward(g):
        rows = pl.ds(g * G, G)
        return remote(arow.at[1, rows], arow.at[2, rows], ws.at[4 + g], wr.at[4 + g], {"col": partner})

    load_x.wait()
    start(both(near, 0, 0))
    start(both(near, 0, 1))
    load_a.wait()
    for g in range(NG):
        row_other(g).start()
    row_partner.start()

    def convert(ref, r0, j):
        hi, lo = split(ref[pl.ds(r0, G), :])
        for k in range(NG):
            arh[j, k, pl.ds(r0, G), :] = hi[:, k * G : (k + 1) * G]
            arl[j, k, pl.ds(r0, G), :] = lo[:, k * G : (k + 1) * G]

    @pl.loop(0, NG)
    def _(g):
        convert(acol.at[0], pl.multiple_of(g * G, G), c)

    row_partner.wait_recv()

    @pl.loop(0, NG)
    def _(g):
        convert(arow.at[0], pl.multiple_of(g * G, G), partner)

    for g in range(NG):
        arrived(both(near, 0, g))
        start(both(far, 0, g))
        if g == 0:
            start(both(near, 0, 2))
        if g == 2:
            start(both(near, 1, 0))
            start(both(near, 1, 1))
        row_other(g).wait_recv()
        row_forward(g).start()
        convert(arow.at[1], g * G, other)
        row_forward(g).wait_recv()
        convert(arow.at[2], g * G, other_partner)

    def block_of(s):
        return (y + jnp.where(s == 1, 3, jnp.where(s == 2, 1, jnp.where(s == 3, 2, 0)))) % 4

    def split_group(ref, s, g):
        hi, lo = split(ref[s, pl.ds(pl.multiple_of(g * G, G), G), :])
        ch[...] = hi
        cl[...] = lo

    def add_product(out, j, g):
        @pl.loop(0, NG)
        def _(m):
            rows = pl.ds(pl.multiple_of(m * G, G), G)
            out[rows, :] += dot3(arh[j, g, rows, :], arl[j, g, rows, :], ch[...], cl[...], NN)

    def y_step(s, g):
        split_group(xcol, s, g)
        add_product(xo, block_of(s), g)

    xo[...] = jnp.zeros_like(xo)
    a2[...] = jnp.zeros_like(a2)

    @pl.loop(0, 3 * NG)
    def _(n):
        y_step(n // NG, n % NG)

    for g in range(NG):
        arrived(both(far, 0, g))

    @pl.loop(0, NG)
    def _(g):
        y_step(3, g)

    @pl.loop(0, NG)
    def _(m):
        rows = pl.ds(pl.multiple_of(m * G, G), G)
        hi, lo = split(xo[rows, :])
        yh[rows, :] = hi
        yl[rows, :] = lo

    def to_partner(q, g):
        return remote(psend.at[q, g], precv.at[q, g], ps.at[q, g], pr.at[q, g], {"col": partner})

    def to_other(g):
        return remote(pkeep.at[1, g], pzrecv.at[g], zs.at[g], zr.at[g], {"col": other})

    def step(s, g):
        j = block_of(s)
        q = (j // 2 + c // 2) % 2
        mine = (j + c) % 2 == 0
        split_group(acol, s, g)

        def p_tile(m):
            rows = pl.ds(pl.multiple_of(m * G, G), G)
            return rows, dot3(yh[rows, :], yl[rows, :], ch[...], cl[...], NT)

        @pl.when(jnp.logical_not(mine))
        def _():
            @pl.loop(0, NG)
            def _(m):
                rows, value = p_tile(m)
                psend[q, g, rows, :] = value

            to_partner(q, g).start()

        @pl.when(mine)
        def _():
            @pl.loop(0, NG)
            def _(m):
                rows, value = p_tile(m)
                pkeep[q, g, rows, :] = value

        add_product(a2, j, g)

        @pl.when(mine)
        def _():
            to_partner(q, g).wait_recv()

            @pl.loop(0, NG)
            def _(m):
                rows = pl.ds(pl.multiple_of(m * G, G), G)
                pkeep[q, g, rows, :] += precv[q, g, rows, :]

            @pl.when(q == 1)
            def _():
                to_other(g).start()

    @pl.loop(0, NG)
    def _(g):
        step(0, g)

    def near_steps(g):
        @pl.loop(1, 3)
        def _(s):
            step(s, g)

    arrived(both(near, 1, 0))
    start(both(far, 1, 0))
    start(both(near, 1, 2))
    near_steps(0)
    arrived(both(near, 1, 1))
    start(both(far, 1, 1))
    near_steps(1)
    arrived(both(far, 1, 0))
    step(3, 0)
    arrived(both(near, 1, 2))
    start(both(far, 1, 2))
    near_steps(2)
    arrived(both(far, 1, 1))
    step(3, 1)
    arrived(both(far, 1, 2))
    step(3, 2)

    for g in range(NG):
        to_other(g).wait_recv()

        @pl.loop(0, NG)
        def _(m):
            rows = pl.ds(pl.multiple_of(m * G, G), G)
            lanes = slice(g * G, (g + 1) * G)
            xo[rows, lanes] = xcol[0, rows, lanes] + (pkeep[0, g, rows, :] + pzrecv[g, rows, :])

    for arr in range(2):
        for g in range(NG):
            for copy in both(near, arr, g) + both(far, arr, g):
                copy.wait_send()
    row_partner.wait_send()
    for g in range(NG):
        row_other(g).wait_send()
        row_forward(g).wait_send()
        to_partner(0, g).wait_send()
        to_partner(1, g).wait_send()
        to_other(g).wait_send()


def solution(mesh):
    def body(a, x):
        block = jax.ShapeDtypeStruct((N, N), F32)
        vmem = pl.BlockSpec(memory_space=pltpu.VMEM)
        dma = pltpu.SemaphoreType.DMA
        xo, a2 = pl.pallas_call(
            kernel,
            out_shape=(block, block),
            in_specs=[pl.BlockSpec(memory_space=pl.ANY)] * 2,
            out_specs=(vmem, vmem),
            scratch_shapes=[
                pltpu.VMEM((4, N, N), F32),
                pltpu.VMEM((4, N, N), F32),
                pltpu.VMEM((3, N, N), F32),
                pltpu.VMEM((4, NG, N, G), BF),
                pltpu.VMEM((4, NG, N, G), BF),
                pltpu.VMEM((N, N), BF),
                pltpu.VMEM((N, N), BF),
                pltpu.VMEM((G, N), BF),
                pltpu.VMEM((G, N), BF),
                pltpu.VMEM((2, NG, N, G), F32),
                pltpu.VMEM((2, NG, N, G), F32),
                pltpu.VMEM((2, NG, N, G), F32),
                pltpu.VMEM((NG, N, G), F32),
                dma((2,)),
                dma((2, 2, 2, NG)),
                dma((2, 2, 2, NG)),
                dma((7,)),
                dma((7,)),
                dma((2, NG)),
                dma((2, NG)),
                dma((NG,)),
                dma((NG,)),
            ],
            compiler_params=pltpu.CompilerParams(
                collective_id=0, has_side_effects=True, vmem_limit_bytes=67043328
            ),
            cost_estimate=pl.CostEstimate(flops=32614907904, bytes_accessed=9437184, transcendentals=0),
        )(a, x)
        return xo, a2

    spec = P(("eq", "row"), "col")
    return jax.shard_map(
        body, mesh=mesh, in_specs=(spec, spec), out_specs=(spec, spec), check_vma=False
    )
```

time: 418 us -> 183 us (0.44)
  the two profiles are of different devices: /device:TPU:1 before, /device:TPU:25 now
where the time goes in v1:
time: 183 us
  Pallas kernels  178 us (97%)
  local copies, waits for them, and re-layouts  4.78 us (3%)
    pallas_call x1, Pallas kernels, body(): pl.pallas_call(kernel, out_shape=(block, block), in_specs=[pl.BlockSpec(m...  178 us
    unnamed x4, local copies, waits for them, and re-layouts  4.78 us

profile of v1, /device:TPU:25, one launch (start us, length us, event | category | flops | bytes accessed | tf_op | source)
XLA Modules:
  0.0 183.3 jit_solution(11209052473706524381)
XLA Ops:
  0.6 177.8 %shard_map.41 = (f32[768,768]{1,0:T(8,128)}, f32[768,768]{1,0:T(8,128)}) custom-call(f32[768,768]{1,0:T(8,128)} %a_hbm.1, f32[768,768]{1,0:T(8,128)} %x_hbm.1), custom_call_target="tpu_custom_call" | custom-call | flops 32614907904 | bytes 9437184 | tf_op jit(solution)/shard_map/pallas_call | solution.py:311
  178.5 0.0 copy-start
  178.5 3.4 %copy.6 = f32[768,768]{1,0:T(8,128)} copy(f32[768,768]{1,0:T(8,128)} %get-tuple-element.4) | data formatting | bytes 4718592
  181.9 0.0 copy-done
  181.9 1.4 copy.7
Async XLA Ops:
  178.5 3.4 %copy-start = (f32[768,768]{1,0:T(8,128)S(1)}, f32[768,768]{1,0:T(8,128)}, u32[]{:S(2)}) copy-start(f32[768,768]{1,0:T(8,128)} %get-tuple-element.5) | copy-start | bytes 7077892

commit v2 on v1

--- a/solution.py
+++ b/solution.py
@@ -52,6 +52,8 @@
     lsem,
     rs,
     rr,
+    ms,
+    mr,
     ws,
     wr,
     ps,
@@ -61,18 +63,19 @@
 ):
     y = lax.axis_index("row")
     c = lax.axis_index("col")
-    right, left = (y + 1) % 4, (y + 3) % 4
     partner = c + 1 - 2 * (c % 2)
     other = (c + 2) % 4
     other_partner = (partner + 2) % 4
 
-    load_a = pltpu.make_async_copy(a_hbm, acol.at[0], lsem.at[0])
-    load_x = pltpu.make_async_copy(x_hbm, xcol.at[0], lsem.at[1])
+    sign = 1 - 2 * (c % 2)
+    place = ((y - c) * sign + 4) % 4
+    load_a = pltpu.make_async_copy(a_hbm, acol.at[place], lsem.at[0])
+    load_x = pltpu.make_async_copy(x_hbm, xcol.at[place], lsem.at[1])
     load_x.start()
     load_a.start()
 
     barrier = pltpu.get_barrier_semaphore()
-    for where in ({"row": left}, {"row": right}, {"col": partner}, {"col": other}):
+    for where in ({"row": (y + 1) % 4}, {"row": (y + 3) % 4}, {"col": partner}, {"col": other}):
         pl.semaphore_signal(barrier, inc=1, device_id=where, device_id_type=pl.DeviceIdType.MESH)
     pl.semaphore_wait(barrier, 4)
 
@@ -88,27 +91,34 @@
 
     cols = (xcol, acol)
 
+    fwd, bwd = (y + sign + 4) % 4, (y - sign + 4) % 4
+    before, after, across = (place + 3) % 4, (place + 1) % 4, (place + 2) % 4
+    ends = place % 2 == 1
+
+    def ring(arr, d, kind, g, slot, r0, size):
+        rows = pl.ds(r0, size)
+        return remote(
+            cols[arr].at[slot, rows],
+            cols[arr].at[slot, rows],
+            rs.at[arr, d, kind, g],
+            rr.at[arr, d, kind, g],
+            {"row": fwd if d == 0 else bwd},
+        )
+
     def near(arr, d, g):
-        ref = cols[arr]
-        rows = pl.ds(g * G, G)
-        return remote(
-            ref.at[0, rows],
-            ref.at[1 + d, rows],
-            rs.at[arr, d, 0, g],
-            rr.at[arr, d, 0, g],
-            {"row": right if d == 0 else left},
-        )
+        return ring(arr, d, 0, g, place, g * G, G)
 
     def far(arr, d, g):
-        ref = cols[arr]
-        rows = pl.ds(g * G + d * H, H)
-        return remote(
-            ref.at[1 + d, rows],
-            ref.at[3, rows],
-            rs.at[arr, d, 1, g],
-            rr.at[arr, d, 1, g],
-            {"row": right if d == 0 else left},
-        )
+        return ring(arr, d, 1, g, before if d == 0 else after, g * G + d * H, H)
+
+    def near_in(arr, d, g):
+        return ring(arr, d, 0, g, before if d == 0 else after, g * G, G)
+
+    def far_in(arr, d, g):
+        return ring(arr, d, 1, g, across, g * G + d * H, H)
+
+    def whole(g, inward):
+        return ring(0, 0, 1, g, across if inward else before, g * G, G)
 
     def both(make, arr, g):
         return [make(arr, d, g) for d in range(2)]
@@ -121,19 +131,78 @@
         for copy in copies:
             copy.wait_recv()
 
-    row_partner = remote(acol.at[0], arow.at[0], ws.at[0], wr.at[0], {"col": partner})
+    def mate(g):
+        rows = pl.ds(g * G, G)
+        return remote(xcol.at[1, rows], xcol.at[1, rows], ms.at[g], mr.at[g], {"col": partner})
+
+    def x_near(act, g):
+        act(near(0, 0, g))
+
+        @pl.when(place != 1)
+        def _():
+            act(near(0, 1, g))
+
+    def x_far(act, g):
+        @pl.when(ends)
+        def _():
+            for copy in both(far, 0, g):
+                act(copy)
+
+        @pl.when(place == 0)
+        def _():
+            act(whole(g, False))
+
+    def x_near_in(g):
+        near_in(0, 0, g).wait_recv()
+
+        @pl.when(place != 0)
+        def _():
+            near_in(0, 1, g).wait_recv()
+
+        @pl.when(place == 0)
+        def _():
+            mate(g).wait_recv()
+
+        @pl.when(place == 2)
+        def _():
+            mate(g).start()
+
+    def x_far_in(g):
+        @pl.when(place % 2 == 0)
+        def _():
+            for copy in both(far_in, 0, g):
+                copy.wait_recv()
+
+        @pl.when(place == 1)
+        def _():
+            whole(g, True).wait_recv()
+
+        @pl.when(place == 3)
+        def _():
+            mate(g).wait_recv()
+
+    def begin(copy):
+        copy.start()
+
+    row_partner = remote(acol.at[place], arow.at[0], ws.at[0], wr.at[0], {"col": partner})
 
     def row_other(g):
         rows = pl.ds(g * G, G)
-        return remote(acol.at[0, rows], arow.at[1, rows], ws.at[1 + g], wr.at[1 + g], {"col": other})
+        return remote(acol.at[place, rows], arow.at[1, rows], ws.at[1 + g], wr.at[1 + g], {"col": other})
 
     def row_forward(g):
         rows = pl.ds(g * G, G)
         return remote(arow.at[1, rows], arow.at[2, rows], ws.at[4 + g], wr.at[4 + g], {"col": partner})
 
     load_x.wait()
-    start(both(near, 0, 0))
-    start(both(near, 0, 1))
+    x_near(begin, 0)
+    x_near(begin, 1)
+
+    @pl.when(place == 1)
+    def _():
+        for g in range(NG):
+            mate(g).start()
+
     load_a.wait()
     for g in range(NG):
         row_other(g).start()
@@ -147,7 +216,7 @@
 
     @pl.loop(0, NG)
     def _(g):
-        convert(acol.at[0], pl.multiple_of(g * G, G), c)
+        convert(acol.at[place], pl.multiple_of(g * G, G), c)
 
     row_partner.wait_recv()
 
@@ -156,10 +225,10 @@
         convert(arow.at[0], pl.multiple_of(g * G, G), partner)
 
     for g in range(NG):
-        arrived(both(near, 0, g))
-        start(both(far, 0, g))
+        x_near_in(g)
+        x_far(begin, g)
         if g == 0:
-            start(both(near, 0, 2))
+            x_near(begin, 2)
         if g == 2:
             start(both(near, 1, 0))
             start(both(near, 1, 1))
@@ -170,7 +239,7 @@
         convert(arow.at[2], g * G, other_partner)
 
     def block_of(s):
-        return (y + jnp.where(s == 1, 3, jnp.where(s == 2, 1, jnp.where(s == 3, 2, 0)))) % 4
+        return (c + sign * s + 4) % 4
 
     def split_group(ref, s, g):
         hi, lo = split(ref[s, pl.ds(pl.multiple_of(g * G, G), G), :])
@@ -185,21 +254,39 @@
 
     def y_step(s, g):
         split_group(xcol, s, g)
-        add_product(xo, block_of(s), g)
+        flipped = jnp.logical_and(s == 1, place % 3 == 0)
+
+        @pl.when(jnp.logical_not(flipped))
+        def _():
+            add_product(xo, block_of(s), g)
+
+        @pl.when(flipped)
+        def _():
+            j = block_of(s)
+            lanes = pl.ds(pl.multiple_of(g * G, G), G)
+
+            @pl.loop(0, NG)
+            def _(m):
+                rows = pl.ds(pl.multiple_of(m * G, G), G)
+                total = xo[rows, lanes]
+                for k in range(NG):
+                    part = slice(k * G, (k + 1) * G)
+                    total += dot3(arh[j, k, rows, :], arl[j, k, rows, :], ch[:, part], cl[:, part], NT)
+                xo[rows, lanes] = total
 
     xo[...] = jnp.zeros_like(xo)
     a2[...] = jnp.zeros_like(a2)
 
     @pl.loop(0, 3 * NG)
     def _(n):
-        y_step(n // NG, n % NG)
-
-    for g in range(NG):
-        arrived(both(far, 0, g))
+        y_step((place + 3 + n // NG) % 4, n % NG)
+
+    for g in range(NG):
+        x_far_in(g)
 
     @pl.loop(0, NG)
     def _(g):
-        y_step(3, g)
+        y_step(across, g)
 
     @pl.loop(0, NG)
     def _(m):
@@ -257,29 +344,29 @@
 
     @pl.loop(0, NG)
     def _(g):
-        step(0, g)
+        step(place, g)
 
     def near_steps(g):
-        @pl.loop(1, 3)
-        def _(s):
-            step(s, g)
-
-    arrived(both(near, 1, 0))
+        @pl.loop(0, 2)
+        def _(n):
+            step((place + 3 + 2 * n) % 4, g)
+
+    arrived(both(near_in, 1, 0))
     start(both(far, 1, 0))
     start(both(near, 1, 2))
     near_steps(0)
-    arrived(both(near, 1, 1))
+    arrived(both(near_in, 1, 1))
     start(both(far, 1, 1))
     near_steps(1)
-    arrived(both(far, 1, 0))
-    step(3, 0)
-    arrived(both(near, 1, 2))
+    arrived(both(far_in, 1, 0))
+    step(across, 0)
+    arrived(both(near_in, 1, 2))
     start(both(far, 1, 2))
     near_steps(2)
-    arrived(both(far, 1, 1))
-    step(3, 1)
-    arrived(both(far, 1, 2))
-    step(3, 2)
+    arrived(both(far_in, 1, 1))
+    step(across, 1)
+    arrived(both(far_in, 1, 2))
+    step(across, 2)
 
     for g in range(NG):
         to_other(g).wait_recv()
@@ -288,12 +375,22 @@
         def _(m):
             rows = pl.ds(pl.multiple_of(m * G, G), G)
             lanes = slice(g * G, (g + 1) * G)
-            xo[rows, lanes] = xcol[0, rows, lanes] + (pkeep[0, g, rows, :] + pzrecv[g, rows, :])
-
-    for arr in range(2):
+            xo[rows, lanes] = xcol[place, rows, lanes] + (pkeep[0, g, rows, :] + pzrecv[g, rows, :])
+
+    def sent(copy):
+        copy.wait_send()
+
+    for g in range(NG):
+        x_near(sent, g)
+        x_far(sent, g)
+        for copy in both(near, 1, g) + both(far, 1, g):
+            copy.wait_send()
+
+    @pl.when(jnp.logical_or(place == 1, place == 2))
+    def _():
         for g in range(NG):
-            for copy in both(near, arr, g) + both(far, arr, g):
-                copy.wait_send()
+            mate(g).wait_send()
+
     row_partner.wait_send()
     for g in range(NG):
         row_other(g).wait_send()
@@ -330,6 +427,8 @@
                 dma((2,)),
                 dma((2, 2, 2, NG)),
                 dma((2, 2, 2, NG)),
+                dma((NG,)),
+                dma((NG,)),
                 dma((7,)),
                 dma((7,)),
                 dma((2, NG)),

time: 183 us -> 178 us (0.973)
  the two profiles are of different devices: /device:TPU:25 before, /device:TPU:22 now
where the time goes in v2:
time: 178 us
  Pallas kernels  173 us (97%)
  local copies, waits for them, and re-layouts  4.78 us (3%)
    pallas_call x1, Pallas kernels, body(): pl.pallas_call(kernel, out_shape=(block, block), in_specs=[pl.BlockSpec(m...  173 us
    unnamed x4, local copies, waits for them, and re-layouts  4.78 us

profile of v2, /device:TPU:22, one launch (start us, length us, event | category | flops | bytes accessed | tf_op | source)
XLA Modules:
  0.0 178.0 jit_solution(9008137942129582575)
XLA Ops:
  0.6 172.6 %shard_map.41 = (f32[768,768]{1,0:T(8,128)}, f32[768,768]{1,0:T(8,128)}) custom-call(f32[768,768]{1,0:T(8,128)} %a_hbm.1, f32[768,768]{1,0:T(8,128)} %x_hbm.1), custom_call_target="tpu_custom_call" | custom-call | flops 32614907904 | bytes 9437184 | tf_op jit(solution)/shard_map/pallas_call | solution.py:408
  173.2 0.0 copy-start
  173.2 3.4 %copy.6 = f32[768,768]{1,0:T(8,128)} copy(f32[768,768]{1,0:T(8,128)} %get-tuple-element.4) | data formatting | bytes 4718592
  176.6 0.0 copy-done
  176.6 1.4 copy.7
Async XLA Ops:
  173.2 3.4 %copy-start = (f32[768,768]{1,0:T(8,128)S(1)}, f32[768,768]{1,0:T(8,128)}, u32[]{:S(2)}) copy-start(f32[768,768]{1,0:T(8,128)} %get-tuple-element.5) | copy-start | bytes 7077892

commit v3 on v2

v3 whole, which is shorter than its diff:
```python
import jax
import jax.numpy as jnp
from jax import lax
from jax.experimental import pallas as pl
from jax.experimental.pallas import tpu as pltpu
from jax.sharding import PartitionSpec as P

N = 768
G = 256
NG = N // G
H = G // 2
NU = 2 * NG
BF = jnp.bfloat16
F32 = jnp.float32


def split(x):
    hi = x.astype(BF)
    lo = (x - hi.astype(F32)).astype(BF)
    return hi, lo


def dot(a, b, contract):
    return lax.dot_general(a, b, (contract, ((), ())), preferred_element_type=F32)


def dot3(ah, al, bh, bl, contract):
    return dot(ah, bh, contract) + (dot(ah, bl, contract) + dot(al, bh, contract))


NN = ((1,), (0,))
NT = ((1,), (1,))


def kernel(
    a_hbm,
    x_hbm,
    xo_hbm,
    a2_hbm,
    xo,
    a2,
    xcol,
    acol,
    arow,
    arh,
    arl,
    yh,
    yl,
    ch,
    cl,
    part,
    precv,
    pzrecv,
    lsem,
    osem,
    rs,
    rr,
    ns,
    nr,
    ms,
    mr,
    ws,
    wr,
    ps,
    pr,
    zs,
    zr,
):
    y = lax.axis_index("row")
    c = lax.axis_index("col")
    partner = c + 1 - 2 * (c % 2)
    other = (c + 2) % 4
    other_partner = (partner + 2) % 4

    sign = 1 - 2 * (c % 2)
    place = ((y - c) * sign + 4) % 4
    load_a = pltpu.make_async_copy(a_hbm, acol.at[place], lsem.at[0])
    load_x = pltpu.make_async_copy(x_hbm, xcol.at[place], lsem.at[1])
    load_x.start()
    load_a.start()

    barrier = pltpu.get_barrier_semaphore()
    for where in ({"row": (y + 1) % 4}, {"row": (y + 3) % 4}, {"col": partner}, {"col": other}):
        pl.semaphore_signal(barrier, inc=1, device_id=where, device_id_type=pl.DeviceIdType.MESH)
    pl.semaphore_wait(barrier, 4)

    def remote(src, dst, send, recv, where):
        return pltpu.make_async_remote_copy(
            src_ref=src,
            dst_ref=dst,
            send_sem=send,
            recv_sem=recv,
            device_id=where,
            device_id_type=pl.DeviceIdType.MESH,
        )

    fwd, bwd = (y + sign + 4) % 4, (y - sign + 4) % 4
    before, after, across = (place + 3) % 4, (place + 1) % 4, (place + 2) % 4

    def ring(d, kind, g, slot, r0, size):
        rows = xcol.at[slot, pl.ds(r0, size)]
        return remote(rows, rows, rs.at[d, kind, g], rr.at[d, kind, g], {"row": fwd if d == 0 else bwd})

    def near(d, g):
        return ring(d, 0, g, place, g * G, G)

    def far(d, g):
        return ring(d, 1, g, before if d == 0 else after, g * G + d * H, H)

    def near_in(d, g):
        return ring(d, 0, g, before if d == 0 else after, g * G, G)

    def far_in(d, g):
        return ring(d, 1, g, across, g * G + d * H, H)

    def whole(g, inward):
        return ring(1, 1, g, across if inward else after, g * G, G)

    def a_ring(d, i, slot):
        half = (d + c + (i % 4) // 2) % 2
        r0 = pl.multiple_of(half * (NG * H), H) + (i % 2) * G
        rows = acol.at[slot, pl.ds(r0, G - (i % 2) * H)]
        return remote(rows, rows, ns.at[d, i], nr.at[d, i], {"row": fwd if d == 0 else bwd})

    def a_out(i):
        slots = (before, after) if i >= 4 else (place, place)
        return [a_ring(d, i, slots[d]) for d in range(2)]

    def a_in(i):
        slots = (across, across) if i >= 4 else (before, after)
        return [a_ring(d, i, slots[d]) for d in range(2)]

    def both(make, g):
        return [make(d, g) for d in range(2)]

    def start(copies):
        for copy in copies:
            copy.start()

    def arrived(copies):
        for copy in copies:
            copy.wait_recv()

    def mate(g):
        rows = pl.ds(g * G, G)
        return remote(xcol.at[1, rows], xcol.at[1, rows], ms.at[g], mr.at[g], {"col": partner})

    def x_near(act, g):
        act(near(0, g))

        @pl.when(place != 1)
        def _():
            act(near(1, g))

    def x_far(act, g):
        @pl.when(place < 2)
        def _():
            act(far(0, g))

        @pl.when(place >= 2)
        def _():
            act(far(1, g))

        @pl.when(place == 1)
        def _():
            act(whole(g, False))

    def x_near_in(g):
        near_in(0, g).wait_recv()

        @pl.when(place != 0)
        def _():
            near_in(1, g).wait_recv()

        @pl.when(place == 0)
        def _():
            mate(g).wait_recv()

        @pl.when(place == 2)
        def _():
            mate(g).start()

    def x_far_in(g):
        @pl.when(jnp.logical_or(place == 1, place == 2))
        def _():
            for copy in both(far_in, g):
                copy.wait_recv()

        @pl.when(place == 0)
        def _():
            whole(g, True).wait_recv()

        @pl.when(place == 3)
        def _():
            mate(g).wait_recv()

    def begin(copy):
        copy.start()

    row_partner = remote(acol.at[place], arow.at[0], ws.at[0], wr.at[0], {"col": partner})

    def row_other(g):
        rows = pl.ds(g * G, G)
        return remote(acol.at[place, rows], arow.at[1, rows], ws.at[1 + g], wr.at[1 + g], {"col": other})

    def row_forward(g):
        rows = pl.ds(g * G, G)
        return remote(arow.at[1, rows], arow.at[2, rows], ws.at[4 + g], wr.at[4 + g], {"col": partner})

    load_x.wait()
    for g in range(NG):
        x_near(begin, g)

    @pl.when(place == 1)
    def _():
        for g in range(NG):
            mate(g).start()

    load_a.wait()
    for g in range(NG):
        row_other(g).start()
    row_partner.start()

    def convert(ref, r0, j):
        hi, lo = split(ref[pl.ds(r0, G), :])
        for k in range(NU):
            arh[j, k, pl.ds(r0, G), :] = hi[:, k * H : (k + 1) * H]
            arl[j, k, pl.ds(r0, G), :] = lo[:, k * H : (k + 1) * H]

    @pl.loop(0, NG)
    def _(g):
        convert(acol.at[place], pl.multiple_of(g * G, G), c)

    row_partner.wait_recv()

    @pl.loop(0, NG)
    def _(g):
        convert(arow.at[0], pl.multiple_of(g * G, G), partner)

    def block_of(s):
        return (c + sign * s + 4) % 4

    def pair(ref, j, u):
        return jnp.concatenate([ref[j, u[0]], ref[j, u[1]]], axis=1)

    def split_unit(ref, s, u, at):
        hi, lo = split(ref[s, pl.ds(pl.multiple_of(u * H, H), H), :])
        ch[at * H : (at + 1) * H, :] = hi
        cl[at * H : (at + 1) * H, :] = lo

    def split_units(ref, s, u):
        split_unit(ref, s, u[0], 0)
        split_unit(ref, s, u[1], 1)

    def lanes_of(n):
        return pl.ds(pl.multiple_of(n * G, G), G)

    def add_product(out, j, u):
        @pl.loop(0, NG)
        def _(n):
            lanes = lanes_of(n)
            out[:, lanes] += dot3(pair(arh, j, u), pair(arl, j, u), ch[:, lanes], cl[:, lanes], NN)

    def y_step(s, g):
        with jax.named_scope("y"):
            u = (2 * g, 2 * g + 1)
            split_units(xcol, s, u)
            flipped = jnp.logical_and(s == 1, place % 3 == 0)
            j = block_of(s)

            @pl.when(jnp.logical_not(flipped))
            def _():
                add_product(xo, j, u)

            @pl.when(flipped)
            def _():
                @pl.loop(0, NG)
                def _(k):
                    v = (2 * k, 2 * k + 1)
                    lanes = lanes_of(k)
                    xo[:, lanes_of(g)] += dot3(pair(arh, j, v), pair(arl, j, v), ch[:, lanes], cl[:, lanes], NT)

    def y_near(g):
        @pl.loop(0, 2)
        def _(n):
            y_step((place + 3 + 2 * n) % 4, g)

    def row_in(g):
        with jax.named_scope("row"):
            row_other(g).wait_recv()
            row_forward(g).start()
            convert(arow.at[1], g * G, other)
            row_forward(g).wait_recv()
            convert(arow.at[2], g * G, other_partner)

    xo[...] = jnp.zeros_like(xo)
    a2[...] = jnp.zeros_like(a2)

    with jax.named_scope("x0"):
        x_near_in(0)
    x_far(begin, 0)
    row_in(0)
    with jax.named_scope("x1"):
        x_near_in(1)
    x_far(begin, 1)
    row_in(1)
    row_in(2)

    with jax.named_scope("x2"):
        x_near_in(2)
    x_far(begin, 2)

    heavy = place // 2

    def a_begin(which):
        for d in range(2):

            @pl.when(which == d)
            def _():
                a_ring(d, 0, place).start()
                a_ring(d, 1, place).start()

    a_begin(heavy)

    @pl.loop(0, NG)
    def _(g):
        y_step(place, g)

    y_near(0)
    a_begin(1 - heavy)

    @pl.loop(1, NG)
    def _(g):
        y_near(g)

    with jax.named_scope("xfar"):
        for g in range(NG):
            x_far_in(g)

    @pl.loop(0, NG)
    def _(g):
        y_step(across, g)

    @pl.loop(0, NG)
    def _(m):
        rows = pl.ds(pl.multiple_of(m * G, G), G)
        hi, lo = split(xo[rows, :])
        yh[rows, :] = hi
        yl[rows, :] = lo

    pieces = ((0, 2), (2, 1), (3, 2), (5, 1))
    low, high, rest = (0, 1), (3, 4), (2, 5)
    left, right = (place + 4 - sign) % 4, (place + 4 + sign) % 4

    def to_partner(q, i):
        u = pl.ds(*pieces[i])
        return remote(part.at[q, u], precv.at[q, u], ps.at[q, i], pr.at[q, i], {"col": partner})

    def to_other(i):
        u = pl.ds(*pieces[i])
        return remote(part.at[3, u], pzrecv.at[u], zs.at[i], zr.at[i], {"col": other})

    def role(s):
        j = block_of(s)
        q = (j // 2 + c // 2) % 2
        return q, (j + c) % 2 == 0

    def partial(s, u):
        with jax.named_scope("p"):
            for k in range(2):
                split_unit(acol, s[k], u[k], k)
            value = dot3(yh[...], yl[...], ch[...], cl[...], NT)
            for k in range(2):
                q, mine = role(s[k])
                part[q + 2 * mine.astype(jnp.int32), u[k]] = value[:, k * H : (k + 1) * H]

    def hand_over(s, i):
        q, mine = role(s)

        @pl.when(jnp.logical_not(mine))
        def _():
            to_partner(q, i).start()

    def collect(s, i):
        q, mine = role(s)
        u0, n = pieces[i]

        @pl.when(mine)
        def _():
            with jax.named_scope("pwait"):
                to_partner(q, i).wait_recv()
            part[2 + q, u0 : u0 + n] += precv[q, u0 : u0 + n]

            @pl.when(q == 1)
            def _():
                to_other(i).start()

    def square(s, u):
        with jax.named_scope("a2"):
            split_units(acol, s, u)
            add_product(a2, block_of(s), u)

    def side(n):
        return (place + 4 + (2 * n - 1) * sign) % 4

    def twice(f):
        @pl.loop(0, 2)
        def _(n):
            f(n)

    def ends(u0):
        return (u0, u0 + 1)

    def over(*items):
        for item in items:
            hand_over(*item)

    def gather(*items):
        for item in items:
            collect(*item)

    def arrive(i):
        with jax.named_scope("ring"):
            arrived(a_in(i))

    twice(lambda n: partial((place, place), ends(3 * n)))
    over((place, 0), (place, 2))
    partial((place, place), rest)
    over((place, 1), (place, 3))
    square(place, low)
    gather((place, 0), (place, 2), (place, 1), (place, 3))
    square(place, high)

    arrive(0)
    start(a_out(4))
    start(a_out(2))
    twice(lambda n: partial((side(n), side(n)), ends(3 * n)))
    over((left, 0), (right, 2))
    square(place, rest)
    gather((left, 0), (right, 2))

    arrive(1)
    start(a_out(5))
    start(a_out(3))
    partial((left, right), rest)
    over((left, 1), (right, 3))
    twice(lambda n: square(side(n), ends(3 * n)))
    gather((left, 1), (right, 3))

    arrive(4)
    twice(lambda n: partial((across, across), ends(3 * n)))
    over((across, 0), (across, 2))
    square(across, low)
    gather((across, 0), (across, 2))
    square(across, high)

    arrive(2)
    twice(lambda n: partial((side(n), side(n)), ends(3 - 3 * n)))
    over((left, 2), (right, 0))
    square(left, high)
    gather((left, 2), (right, 0))

    arrive(5)
    partial((across, across), rest)
    over((across, 1), (across, 3))
    square(right, low)
    gather((across, 1), (across, 3))

    arrive(3)
    partial((left, right), (5, 2))
    over((left, 3), (right, 1))
    square(across, rest)
    gather((left, 3), (right, 1))
    twice(lambda n: square(side(n), rest))

    a2_out = pltpu.make_async_copy(a2, a2_hbm, lsem.at[0])
    a2_out.start()

    def xo_out(i):
        lanes = pl.ds(pieces[i][0] * H, pieces[i][1] * H)
        return pltpu.make_async_copy(xo.at[:, lanes], xo_hbm.at[:, lanes], osem.at[i])

    for i in (0, 2, 1, 3):
        u0, n = pieces[i]
        with jax.named_scope("z"):
            to_other(i).wait_recv()

        for u in range(u0, u0 + n):
            lanes = slice(u * H, (u + 1) * H)
            xo[:, lanes] = xcol[place, :, lanes] + (part[2, u] + pzrecv[u])

        xo_out(i).start()

    def sent(copy):
        copy.wait_send()

    for g in range(NG):
        x_near(sent, g)
        x_far(sent, g)
        row_other(g).wait_send()
        row_forward(g).wait_send()

    for i in range(6):
        for copy in a_out(i):
            copy.wait_send()

    for i in range(4):
        to_partner(0, i).wait_send()
        to_partner(1, i).wait_send()
        to_other(i).wait_send()

    @pl.when(jnp.logical_or(place == 1, place == 2))
    def _():
        for g in range(NG):
            mate(g).wait_send()

    row_partner.wait_send()
    a2_out.wait()
    for i in range(4):
        xo_out(i).wait()


def solution(mesh):
    def body(a, x):
        block = jax.ShapeDtypeStruct((N, N), F32)
        dma = pltpu.SemaphoreType.DMA
        xo, a2 = pl.pallas_call(
            kernel,
            out_shape=(block, block),
            in_specs=[pl.BlockSpec(memory_space=pl.ANY)] * 2,
            out_specs=[pl.BlockSpec(memory_space=pl.ANY)] * 2,
            scratch_shapes=[
                pltpu.VMEM((N, N), F32),
                pltpu.VMEM((N, N), F32),
                pltpu.VMEM((4, N, N), F32),
                pltpu.VMEM((4, N, N), F32),
                pltpu.VMEM((3, N, N), F32),
                pltpu.VMEM((4, NU, N, H), BF),
                pltpu.VMEM((4, NU, N, H), BF),
                pltpu.VMEM((N, N), BF),
                pltpu.VMEM((N, N), BF),
                pltpu.VMEM((G, N), BF),
                pltpu.VMEM((G, N), BF),
                pltpu.VMEM((4, NU, N, H), F32),
                pltpu.VMEM((2, NU, N, H), F32),
                pltpu.VMEM((NU, N, H), F32),
                dma((2,)),
                dma((4,)),
                dma((2, 2, NG)),
                dma((2, 2, NG)),
                dma((2, 6)),
                dma((2, 6)),
                dma((NG,)),
                dma((NG,)),
                dma((7,)),
                dma((7,)),
                dma((2, 4)),
                dma((2, 4)),
                dma((4,)),
                dma((4,)),
            ],
            compiler_params=pltpu.CompilerParams(
                collective_id=0, has_side_effects=True, vmem_limit_bytes=67043328
            ),
            cost_estimate=pl.CostEstimate(flops=32614907904, bytes_accessed=9437184, transcendentals=0),
        )(a, x)
        return xo, a2

    spec = P(("eq", "row"), "col")
    return jax.shard_map(
        body, mesh=mesh, in_specs=(spec, spec), out_specs=(spec, spec), check_vma=False
    )
```

time: 178 us -> 168 us (0.944)
  the two profiles are of different devices: /device:TPU:22 before, /device:TPU:1 now
where the time goes in v3:
time: 168 us; the launch traced here: 167 us
  Pallas kernels  162 us (96%)
  local copies, waits for them, and re-layouts  4.78 us (3%)
    pallas_call x1, Pallas kernels, body(): pl.pallas_call(kernel, out_shape=(block, block), in_specs=[pl.BlockSpec(m...  162 us
    unnamed x4, local copies, waits for them, and re-layouts  4.78 us

profile of v3, /device:TPU:1, one launch (start us, length us, event | category | flops | bytes accessed | tf_op | source)
XLA Modules:
  0.0 167.5 jit_solution(6505950358507443975)
XLA Ops:
  0.6 162.1 %shard_map.41 = (f32[768,768]{1,0:T(8,128)}, f32[768,768]{1,0:T(8,128)}) custom-call(f32[768,768]{1,0:T(8,128)} %a_hbm.1, f32[768,768]{1,0:T(8,128)} %x_hbm.1), custom_call_target="tpu_custom_call" | custom-call | flops 32614907904 | bytes 9437184 | tf_op jit(solution)/shard_map/pallas_call | solution.py:527
  162.7 0.0 copy-start
  162.7 3.4 %copy.6 = f32[768,768]{1,0:T(8,128)} copy(f32[768,768]{1,0:T(8,128)} %get-tuple-element.4) | data formatting | bytes 4718592
  166.1 0.0 copy-done
  166.1 1.4 copy.7
Async XLA Ops:
  162.7 3.4 %copy-start = (f32[768,768]{1,0:T(8,128)S(1)}, f32[768,768]{1,0:T(8,128)}, u32[]{:S(2)}) copy-start(f32[768,768]{1,0:T(8,128)} %get-tuple-element.5) | copy-start | bytes 7077892

commit v4 on v3

--- a/solution.py
+++ b/solution.py
@@ -35,8 +35,6 @@
 def kernel(
     a_hbm,
     x_hbm,
-    xo_hbm,
-    a2_hbm,
     xo,
     a2,
     xcol,
@@ -52,7 +50,6 @@
     precv,
     pzrecv,
     lsem,
-    osem,
     rs,
     rr,
     ns,
@@ -117,17 +114,16 @@
         return ring(1, 1, g, across if inward else after, g * G, G)
 
     def a_ring(d, i, slot):
-        half = (d + c + (i % 4) // 2) % 2
-        r0 = pl.multiple_of(half * (NG * H), H) + (i % 2) * G
-        rows = acol.at[slot, pl.ds(r0, G - (i % 2) * H)]
+        half = (d + c + (1 if 3 <= i < 6 else 0)) % 2
+        rows = acol.at[slot, pl.ds(pl.multiple_of(half * (NG * H), H) + (i % 3) * H, H)]
         return remote(rows, rows, ns.at[d, i], nr.at[d, i], {"row": fwd if d == 0 else bwd})
 
     def a_out(i):
-        slots = (before, after) if i >= 4 else (place, place)
+        slots = (before, after) if i >= 6 else (place, place)
         return [a_ring(d, i, slots[d]) for d in range(2)]
 
     def a_in(i):
-        slots = (across, across) if i >= 4 else (before, after)
+        slots = (across, across) if i >= 6 else (before, after)
         return [a_ring(d, i, slots[d]) for d in range(2)]
 
     def both(make, g):
@@ -317,8 +313,8 @@
 
             @pl.when(which == d)
             def _():
-                a_ring(d, 0, place).start()
-                a_ring(d, 1, place).start()
+                for i in range(3):
+                    a_ring(d, i, place).start()
 
     a_begin(heavy)
 
@@ -348,17 +344,13 @@
         yh[rows, :] = hi
         yl[rows, :] = lo
 
-    pieces = ((0, 2), (2, 1), (3, 2), (5, 1))
-    low, high, rest = (0, 1), (3, 4), (2, 5)
     left, right = (place + 4 - sign) % 4, (place + 4 + sign) % 4
 
-    def to_partner(q, i):
-        u = pl.ds(*pieces[i])
-        return remote(part.at[q, u], precv.at[q, u], ps.at[q, i], pr.at[q, i], {"col": partner})
-
-    def to_other(i):
-        u = pl.ds(*pieces[i])
-        return remote(part.at[3, u], pzrecv.at[u], zs.at[i], zr.at[i], {"col": other})
+    def to_partner(q, u):
+        return remote(part.at[q, u], precv.at[q, u], ps.at[q, u], pr.at[q, u], {"col": partner})
+
+    def to_other(u):
+        return remote(part.at[3, u], pzrecv.at[u], zs.at[u], zr.at[u], {"col": other})
 
     def role(s):
         j = block_of(s)
@@ -374,122 +366,82 @@
                 q, mine = role(s[k])
                 part[q + 2 * mine.astype(jnp.int32), u[k]] = value[:, k * H : (k + 1) * H]
 
-    def hand_over(s, i):
-        q, mine = role(s)
-
-        @pl.when(jnp.logical_not(mine))
-        def _():
-            to_partner(q, i).start()
-
-    def collect(s, i):
-        q, mine = role(s)
-        u0, n = pieces[i]
-
-        @pl.when(mine)
-        def _():
-            with jax.named_scope("pwait"):
-                to_partner(q, i).wait_recv()
-            part[2 + q, u0 : u0 + n] += precv[q, u0 : u0 + n]
-
-            @pl.when(q == 1)
+    def hand_over(s, u):
+        for k in range(2):
+            q, mine = role(s[k])
+
+            @pl.when(jnp.logical_not(mine))
             def _():
-                to_other(i).start()
+                to_partner(q, u[k]).start()
+
+    def collect(s, u):
+        for k in range(2):
+            q, mine = role(s[k])
+
+            @pl.when(mine)
+            def _():
+                with jax.named_scope("pwait"):
+                    to_partner(q, u[k]).wait_recv()
+                part[2 + q, u[k]] += precv[q, u[k]]
+
+                @pl.when(q == 1)
+                def _():
+                    to_other(u[k]).start()
 
     def square(s, u):
         with jax.named_scope("a2"):
             split_units(acol, s, u)
             add_product(a2, block_of(s), u)
 
-    def side(n):
-        return (place + 4 + (2 * n - 1) * sign) % 4
-
-    def twice(f):
-        @pl.loop(0, 2)
-        def _(n):
-            f(n)
-
-    def ends(u0):
-        return (u0, u0 + 1)
-
-    def over(*items):
-        for item in items:
-            hand_over(*item)
-
-    def gather(*items):
-        for item in items:
-            collect(*item)
-
     def arrive(i):
         with jax.named_scope("ring"):
             arrived(a_in(i))
 
-    twice(lambda n: partial((place, place), ends(3 * n)))
-    over((place, 0), (place, 2))
-    partial((place, place), rest)
-    over((place, 1), (place, 3))
-    square(place, low)
-    gather((place, 0), (place, 2), (place, 1), (place, 3))
-    square(place, high)
-
+    def stage(s, u, meanwhile):
+        partial(s, u)
+        hand_over(s, u)
+        square(*meanwhile)
+        collect(s, u)
+
+    own = (place, place)
+    for u in range(3):
+        partial(own, (u, u + 3))
+        hand_over(own, (u, u + 3))
+    square(place, (0, 1))
+    for u in range(3):
+        collect(own, (u, u + 3))
+
+    sides, far_side = (left, right), (across, across)
     arrive(0)
-    start(a_out(4))
-    start(a_out(2))
-    twice(lambda n: partial((side(n), side(n)), ends(3 * n)))
-    over((left, 0), (right, 2))
-    square(place, rest)
-    gather((left, 0), (right, 2))
-
+    start(a_out(6))
+    stage(sides, (0, 3), (place, (2, 3)))
     arrive(1)
-    start(a_out(5))
-    start(a_out(3))
-    partial((left, right), rest)
-    over((left, 1), (right, 3))
-    twice(lambda n: square(side(n), ends(3 * n)))
-    gather((left, 1), (right, 3))
-
+    start(a_out(7))
+    stage(sides, (1, 4), (place, (4, 5)))
+    arrive(2)
+    for i in (8, 3, 4, 5):
+        start(a_out(i))
+    stage(sides, (2, 5), (left, (0, 1)))
+    arrive(6)
+    stage(far_side, (0, 3), (right, (3, 4)))
+    arrive(7)
+    stage(far_side, (1, 4), (across, (0, 3)))
+    arrive(8)
+    stage(far_side, (2, 5), (across, (1, 4)))
+    arrive(3)
+    stage(sides, (3, 0), (across, (2, 5)))
+    square(left, (2, 3))
     arrive(4)
-    twice(lambda n: partial((across, across), ends(3 * n)))
-    over((across, 0), (across, 2))
-    square(across, low)
-    gather((across, 0), (across, 2))
-    square(across, high)
-
-    arrive(2)
-    twice(lambda n: partial((side(n), side(n)), ends(3 - 3 * n)))
-    over((left, 2), (right, 0))
-    square(left, high)
-    gather((left, 2), (right, 0))
-
+    stage(sides, (4, 1), (right, (5, 0)))
     arrive(5)
-    partial((across, across), rest)
-    over((across, 1), (across, 3))
-    square(right, low)
-    gather((across, 1), (across, 3))
-
-    arrive(3)
-    partial((left, right), (5, 2))
-    over((left, 3), (right, 1))
-    square(across, rest)
-    gather((left, 3), (right, 1))
-    twice(lambda n: square(side(n), rest))
-
-    a2_out = pltpu.make_async_copy(a2, a2_hbm, lsem.at[0])
-    a2_out.start()
-
-    def xo_out(i):
-        lanes = pl.ds(pieces[i][0] * H, pieces[i][1] * H)
-        return pltpu.make_async_copy(xo.at[:, lanes], xo_hbm.at[:, lanes], osem.at[i])
-
-    for i in (0, 2, 1, 3):
-        u0, n = pieces[i]
+    stage(sides, (5, 2), (left, (4, 5)))
+    square(right, (1, 2))
+
+    for u in (0, 3, 1, 4, 2, 5):
         with jax.named_scope("z"):
-            to_other(i).wait_recv()
-
-        for u in range(u0, u0 + n):
-            lanes = slice(u * H, (u + 1) * H)
-            xo[:, lanes] = xcol[place, :, lanes] + (part[2, u] + pzrecv[u])
-
-        xo_out(i).start()
+            to_other(u).wait_recv()
+        lanes = slice(u * H, (u + 1) * H)
+        xo[:, lanes] = xcol[place, :, lanes] + (part[2, u] + pzrecv[u])
 
     def sent(copy):
         copy.wait_send()
@@ -500,14 +452,14 @@
         row_other(g).wait_send()
         row_forward(g).wait_send()
 
-    for i in range(6):
+    for i in range(9):
         for copy in a_out(i):
             copy.wait_send()
 
-    for i in range(4):
-        to_partner(0, i).wait_send()
-        to_partner(1, i).wait_send()
-        to_other(i).wait_send()
+    for u in range(NU):
+        to_partner(0, u).wait_send()
+        to_partner(1, u).wait_send()
+        to_other(u).wait_send()
 
     @pl.when(jnp.logical_or(place == 1, place == 2))
     def _():
@@ -515,23 +467,18 @@
             mate(g).wait_send()
 
     row_partner.wait_send()
-    a2_out.wait()
-    for i in range(4):
-        xo_out(i).wait()
 
 
 def solution(mesh):
     def body(a, x):
-        block = jax.ShapeDtypeStruct((N, N), F32)
+        block = pltpu.VMEM((N, N), F32)
         dma = pltpu.SemaphoreType.DMA
         xo, a2 = pl.pallas_call(
             kernel,
             out_shape=(block, block),
             in_specs=[pl.BlockSpec(memory_space=pl.ANY)] * 2,
-            out_specs=[pl.BlockSpec(memory_space=pl.ANY)] * 2,
+            out_specs=[pl.BlockSpec(memory_space=pltpu.VMEM)] * 2,
             scratch_shapes=[
-                pltpu.VMEM((N, N), F32),
-                pltpu.VMEM((N, N), F32),
                 pltpu.VMEM((4, N, N), F32),
                 pltpu.VMEM((4, N, N), F32),
                 pltpu.VMEM((3, N, N), F32),
@@ -545,22 +492,21 @@
                 pltpu.VMEM((2, NU, N, H), F32),
                 pltpu.VMEM((NU, N, H), F32),
                 dma((2,)),
-                dma((4,)),
                 dma((2, 2, NG)),
                 dma((2, 2, NG)),
-                dma((2, 6)),
-                dma((2, 6)),
+                dma((2, 9)),
+                dma((2, 9)),
                 dma((NG,)),
                 dma((NG,)),
                 dma((7,)),
                 dma((7,)),
-                dma((2, 4)),
-                dma((2, 4)),
-                dma((4,)),
-                dma((4,)),
+                dma((2, NU)),
+                dma((2, NU)),
+                dma((NU,)),
+                dma((NU,)),
             ],
             compiler_params=pltpu.CompilerParams(
-                collective_id=0, has_side_effects=True, vmem_limit_bytes=67043328
+                collective_id=0, has_side_effects=True, vmem_limit_bytes=57 * 2**20
             ),
             cost_estimate=pl.CostEstimate(flops=32614907904, bytes_accessed=9437184, transcendentals=0),
         )(a, x)

time: 168 us -> 162 us (0.964)
  Pallas kernels: 162 us -> 158 us
  local copies, waits for them, and re-layouts: 4.78 us -> 2.81 us
    pallas_call x1, Pallas kernels: 162 us -> 158 us  [body(): pl.pallas_call(kernel, out_shape=(block, block), in_specs=[pl.BlockSpec(m...]
    unnamed x4 -> x2, local copies, waits for them, and re-layouts: 4.78 us -> 2.81 us
where the time goes in v4:
time: 162 us; the launch traced here: 161 us
  Pallas kernels  158 us (98%)
  local copies, waits for them, and re-layouts  2.81 us (2%)
    pallas_call x1, Pallas kernels, body(): pl.pallas_call(kernel, out_shape=(block, block), in_specs=[pl.BlockSpec(m...  158 us

profile of v4, /device:TPU:1, one launch (start us, length us, event | category | flops | bytes accessed | tf_op | source)
XLA Modules:
  0.0 161.5 jit_solution(8128212107633691814)
XLA Ops:
  0.6 158.0 %shard_map.41 = (f32[768,768]{1,0:T(8,128)S(1)}, f32[768,768]{1,0:T(8,128)S(1)}) custom-call(f32[768,768]{1,0:T(8,128)} %a_hbm.1, f32[768,768]{1,0:T(8,128)} %x_hbm.1), custom_call_target="tpu_custom_call" | custom-call | flops 32614907904 | bytes 9437184 | tf_op jit(solution)/shard_map/pallas_call | solution.py:476
  158.7 1.4 copy.6
  160.1 1.4 copy.7

commit v5 on v4

--- a/solution.py
+++ b/solution.py
@@ -49,6 +49,7 @@
     part,
     precv,
     pzrecv,
+    zx,
     lsem,
     rs,
     rr,
@@ -56,6 +57,8 @@
     nr,
     ms,
     mr,
+    cs,
+    cr,
     ws,
     wr,
     ps,
@@ -77,9 +80,9 @@
     load_a.start()
 
     barrier = pltpu.get_barrier_semaphore()
-    for where in ({"row": (y + 1) % 4}, {"row": (y + 3) % 4}, {"col": partner}, {"col": other}):
+    for where in ({"row": (y + 1) % 4}, {"row": (y + 3) % 4}, {"col": partner}, {"col": other}, {"col": other_partner}):
         pl.semaphore_signal(barrier, inc=1, device_id=where, device_id_type=pl.DeviceIdType.MESH)
-    pl.semaphore_wait(barrier, 4)
+    pl.semaphore_wait(barrier, 5)
 
     def remote(src, dst, send, recv, where):
         return pltpu.make_async_remote_copy(
@@ -94,24 +97,39 @@
     fwd, bwd = (y + sign + 4) % 4, (y - sign + 4) % 4
     before, after, across = (place + 3) % 4, (place + 1) % 4, (place + 2) % 4
 
-    def ring(d, kind, g, slot, r0, size):
-        rows = xcol.at[slot, pl.ds(r0, size)]
-        return remote(rows, rows, rs.at[d, kind, g], rr.at[d, kind, g], {"row": fwd if d == 0 else bwd})
-
-    def near(d, g):
-        return ring(d, 0, g, place, g * G, G)
-
-    def far(d, g):
-        return ring(d, 1, g, before if d == 0 else after, g * G + d * H, H)
-
-    def near_in(d, g):
-        return ring(d, 0, g, before if d == 0 else after, g * G, G)
-
-    def far_in(d, g):
-        return ring(d, 1, g, across, g * G + d * H, H)
-
-    def whole(g, inward):
-        return ring(1, 1, g, across if inward else after, g * G, G)
+    def ring(d, kind, g, slot, half):
+        r0, size = (g * G, G) if half is None else (g * G + half * H, H)
+        part = xcol.at[slot, pl.ds(r0, size), pl.ds(0, (g + 1) * G if slot == 0 else N)]
+        return remote(part, part, rs.at[d, kind, g], rr.at[d, kind, g], {"row": fwd if d == 0 else bwd})
+
+    def near_of(p, g):
+        go = []
+        if p != 3 or g > 0:
+            go.append((0, 0, g, p, None))
+        if p != 1:
+            go.append((1, 0, g, p, None))
+        return go
+
+    def far_of(p, g):
+        if p == 0:
+            return ((), ((0, 1, g, 3, 0),), ((0, 1, g, 3, None),))[g]
+        if p == 1:
+            return ((0, 1, g, 0, 0 if g == 2 else None), (1, 1, g, 2, None))
+        if p == 2:
+            return (((1, 1, g, 3, None),), ((1, 1, g, 3, 1),), ())[g]
+        return ((1, 1, g, 0, 1),) if g == 2 else ()
+
+    def into(table, p, g):
+        return [t for t in table((p + 3) % 4, g) if t[0] == 0] + [
+            t for t in table((p + 1) % 4, g) if t[0] == 1
+        ]
+
+    def each_place(f):
+        for p in range(4):
+
+            @pl.when(place == p)
+            def _():
+                f(p)
 
     def a_ring(d, i, slot):
         half = (d + c + (1 if 3 <= i < 6 else 0)) % 2
@@ -141,54 +159,40 @@
         rows = pl.ds(g * G, G)
         return remote(xcol.at[1, rows], xcol.at[1, rows], ms.at[g], mr.at[g], {"col": partner})
 
+    def corner():
+        return remote(xcol.at[3, :, pl.ds(0, G)], zx, cs.at[0], cr.at[0], {"col": other_partner})
+
     def x_near(act, g):
-        act(near(0, g))
-
-        @pl.when(place != 1)
-        def _():
-            act(near(1, g))
+        each_place(lambda p: [act(ring(*t)) for t in near_of(p, g)])
 
     def x_far(act, g):
-        @pl.when(place < 2)
-        def _():
-            act(far(0, g))
-
-        @pl.when(place >= 2)
-        def _():
-            act(far(1, g))
-
-        @pl.when(place == 1)
-        def _():
-            act(whole(g, False))
+        each_place(lambda p: [act(ring(*t)) for t in far_of(p, g)])
 
     def x_near_in(g):
-        near_in(0, g).wait_recv()
-
-        @pl.when(place != 0)
-        def _():
-            near_in(1, g).wait_recv()
-
-        @pl.when(place == 0)
-        def _():
-            mate(g).wait_recv()
-
-        @pl.when(place == 2)
-        def _():
-            mate(g).start()
+        def land(p):
+            for t in into(near_of, p, g):
+                ring(*t).wait_recv()
+            if p == 0:
+                mate(g).wait_recv()
+            if p == 2:
+                mate(g).start()
+
+        each_place(land)
 
     def x_far_in(g):
-        @pl.when(jnp.logical_or(place == 1, place == 2))
-        def _():
-            for copy in both(far_in, g):
-                copy.wait_recv()
-
-        @pl.when(place == 0)
-        def _():
-            whole(g, True).wait_recv()
-
-        @pl.when(place == 3)
-        def _():
-            mate(g).wait_recv()
+        def land(p):
+            for t in into(far_of, p, g):
+                ring(*t).wait_recv()
+            if p == 3:
+                mate(g).wait_recv()
+
+        each_place(land)
+
+    def mirror():
+        for g, h in ((0, 1), (0, 2), (1, 2)):
+            xcol[0, g * G : (g + 1) * G, h * G : (h + 1) * G] = xcol[
+                0, h * G : (h + 1) * G, g * G : (g + 1) * G
+            ].T
 
     def begin(copy):
         copy.start()
@@ -216,6 +220,11 @@
     for g in range(NG):
         row_other(g).start()
     row_partner.start()
+
+    @pl.when(place == 3)
+    def _():
+        corner().start()
+
 
     def convert(ref, r0, j):
         hi, lo = split(ref[pl.ds(r0, G), :])
@@ -300,30 +309,30 @@
         x_near_in(1)
     x_far(begin, 1)
     row_in(1)
-    row_in(2)
-
     with jax.named_scope("x2"):
         x_near_in(2)
     x_far(begin, 2)
-
-    heavy = place // 2
-
-    def a_begin(which):
-        for d in range(2):
-
-            @pl.when(which == d)
+    row_in(2)
+
+    def a_begin(late):
+        for d, p in ((0, 3), (1, 0)):
+
+            @pl.when((place == p) == late)
             def _():
                 for i in range(3):
                     a_ring(d, i, place).start()
 
-    a_begin(heavy)
+    a_begin(False)
+
+    @pl.when(place % 2 == 1)
+    def _():
+        mirror()
 
     @pl.loop(0, NG)
     def _(g):
         y_step(place, g)
 
-    y_near(0)
-    a_begin(1 - heavy)
+    a_begin(True)
 
     @pl.loop(1, NG)
     def _(g):
@@ -332,6 +341,17 @@
     with jax.named_scope("xfar"):
         for g in range(NG):
             x_far_in(g)
+
+        @pl.when(place == 2)
+        def _():
+            mirror()
+
+        @pl.when(place == 0)
+        def _():
+            corner().wait_recv()
+            xcol[3, :G, :] = zx[...].T
+
+    y_near(0)
 
     @pl.loop(0, NG)
     def _(g):
@@ -403,6 +423,8 @@
         square(*meanwhile)
         collect(s, u)
 
+    arrive(0)
+    start(a_out(6))
     own = (place, place)
     for u in range(3):
         partial(own, (u, u + 3))
@@ -412,8 +434,6 @@
         collect(own, (u, u + 3))
 
     sides, far_side = (left, right), (across, across)
-    arrive(0)
-    start(a_out(6))
     stage(sides, (0, 3), (place, (2, 3)))
     arrive(1)
     start(a_out(7))
@@ -466,6 +486,10 @@
         for g in range(NG):
             mate(g).wait_send()
 
+    @pl.when(place == 3)
+    def _():
+        corner().wait_send()
+
     row_partner.wait_send()
 
 
@@ -491,6 +515,7 @@
                 pltpu.VMEM((4, NU, N, H), F32),
                 pltpu.VMEM((2, NU, N, H), F32),
                 pltpu.VMEM((NU, N, H), F32),
+                pltpu.VMEM((N, G), F32),
                 dma((2,)),
                 dma((2, 2, NG)),
                 dma((2, 2, NG)),
@@ -498,6 +523,8 @@
                 dma((2, 9)),
                 dma((NG,)),
                 dma((NG,)),
+                dma((1,)),
+                dma((1,)),
                 dma((7,)),
                 dma((7,)),
                 dma((2, NU)),

time: 162 us -> 156 us (0.963)
  Pallas kernels: 158 us -> 152 us
    pallas_call x1, Pallas kernels: 158 us -> 152 us  [body(): pl.pallas_call(kernel, out_shape=(block, block), in_specs=[pl.BlockSpec(m...]
where the time goes in v5:
time: 156 us
  Pallas kernels  152 us (97%)
  local copies, waits for them, and re-layouts  2.81 us (2%)
    pallas_call x1, Pallas kernels, body(): pl.pallas_call(kernel, out_shape=(block, block), in_specs=[pl.BlockSpec(m...  152 us

profile of v5, /device:TPU:1, one launch (start us, length us, event | category | flops | bytes accessed | tf_op | source)
XLA Modules:
  0.0 155.7 jit_solution(7774825725978370236)
XLA Ops:
  0.6 152.2 %shard_map.41 = (f32[768,768]{1,0:T(8,128)S(1)}, f32[768,768]{1,0:T(8,128)S(1)}) custom-call(f32[768,768]{1,0:T(8,128)} %a_hbm.1, f32[768,768]{1,0:T(8,128)} %x_hbm.1), custom_call_target="tpu_custom_call" | custom-call | flops 32614907904 | bytes 9437184 | tf_op jit(solution)/shard_map/pallas_call | solution.py:500
  152.8 1.4 copy.6
  154.3 1.4 copy.7

commit v6 on v5

--- a/solution.py
+++ b/solution.py
@@ -199,6 +199,14 @@
 
     row_partner = remote(acol.at[place], arow.at[0], ws.at[0], wr.at[0], {"col": partner})
 
+    def a_begin(d, units, where):
+        for p in where:
+
+            @pl.when(place == p)
+            def _():
+                for i in units:
+                    a_ring(d, i, p).start()
+
     def row_other(g):
         rows = pl.ds(g * G, G)
         return remote(acol.at[place, rows], arow.at[1, rows], ws.at[1 + g], wr.at[1 + g], {"col": other})
@@ -220,6 +228,8 @@
     for g in range(NG):
         row_other(g).start()
     row_partner.start()
+
+    a_begin(0, (0, 1, 2), (0,))
 
     @pl.when(place == 3)
     def _():
@@ -260,8 +270,8 @@
     def lanes_of(n):
         return pl.ds(pl.multiple_of(n * G, G), G)
 
-    def add_product(out, j, u):
-        @pl.loop(0, NG)
+    def add_product(out, j, u, unroll=False):
+        @pl.loop(0, NG, unroll=unroll)
         def _(n):
             lanes = lanes_of(n)
             out[:, lanes] += dot3(pair(arh, j, u), pair(arl, j, u), ch[:, lanes], cl[:, lanes], NN)
@@ -275,7 +285,7 @@
 
             @pl.when(jnp.logical_not(flipped))
             def _():
-                add_product(xo, j, u)
+                add_product(xo, j, u, True)
 
             @pl.when(flipped)
             def _():
@@ -290,6 +300,10 @@
         def _(n):
             y_step((place + 3 + 2 * n) % 4, g)
 
+    def arrive(i):
+        with jax.named_scope("ring"):
+            arrived(a_in(i))
+
     def row_in(g):
         with jax.named_scope("row"):
             row_other(g).wait_recv()
@@ -308,21 +322,20 @@
     with jax.named_scope("x1"):
         x_near_in(1)
     x_far(begin, 1)
+    a_begin(0, (0,), (1, 2))
+    a_begin(1, (0,), (2, 3))
     row_in(1)
     with jax.named_scope("x2"):
         x_near_in(2)
     x_far(begin, 2)
+
+    a_begin(0, (1, 2), (1, 2))
+    a_begin(1, (0, 1, 2), (1,))
+    a_begin(1, (1, 2), (2, 3))
+    a_begin(1, (0,), (0,))
     row_in(2)
-
-    def a_begin(late):
-        for d, p in ((0, 3), (1, 0)):
-
-            @pl.when((place == p) == late)
-            def _():
-                for i in range(3):
-                    a_ring(d, i, place).start()
-
-    a_begin(False)
+    a_begin(0, (0, 1, 2), (3,))
+    a_begin(1, (1, 2), (0,))
 
     @pl.when(place % 2 == 1)
     def _():
@@ -331,8 +344,6 @@
     @pl.loop(0, NG)
     def _(g):
         y_step(place, g)
-
-    a_begin(True)
 
     @pl.loop(1, NG)
     def _(g):
@@ -352,6 +363,8 @@
             xcol[3, :G, :] = zx[...].T
 
     y_near(0)
+    arrive(0)
+    start(a_out(6))
 
     @pl.loop(0, NG)
     def _(g):
@@ -413,48 +426,52 @@
             split_units(acol, s, u)
             add_product(a2, block_of(s), u)
 
-    def arrive(i):
-        with jax.named_scope("ring"):
-            arrived(a_in(i))
-
-    def stage(s, u, meanwhile):
+    def sums(s, u):
         partial(s, u)
         hand_over(s, u)
+
+    def stage(s, u, meanwhile):
+        sums(s, u)
         square(*meanwhile)
         collect(s, u)
 
-    arrive(0)
-    start(a_out(6))
-    own = (place, place)
-    for u in range(3):
-        partial(own, (u, u + 3))
-        hand_over(own, (u, u + 3))
-    square(place, (0, 1))
-    for u in range(3):
-        collect(own, (u, u + 3))
-
-    sides, far_side = (left, right), (across, across)
-    stage(sides, (0, 3), (place, (2, 3)))
+    own, sides, far_side = (place, place), (left, right), (across, across)
     arrive(1)
     start(a_out(7))
-    stage(sides, (1, 4), (place, (4, 5)))
+    sums(sides, (0, 3))
+    sums(sides, (1, 4))
+    collect(sides, (0, 3))
     arrive(2)
     for i in (8, 3, 4, 5):
         start(a_out(i))
-    stage(sides, (2, 5), (left, (0, 1)))
+    sums(sides, (2, 5))
+    collect(sides, (1, 4))
+    sums(own, (0, 3))
+    collect(sides, (2, 5))
+    sums(own, (1, 4))
+    collect(own, (0, 3))
+    sums(own, (2, 5))
+    collect(own, (1, 4))
     arrive(6)
-    stage(far_side, (0, 3), (right, (3, 4)))
+    sums(far_side, (0, 3))
+    collect(own, (2, 5))
+    square(place, (0, 1))
+    collect(far_side, (0, 3))
+    square(place, (2, 3))
     arrive(7)
-    stage(far_side, (1, 4), (across, (0, 3)))
+    stage(far_side, (1, 4), (place, (4, 5)))
+    square(left, (0, 1))
     arrive(8)
-    stage(far_side, (2, 5), (across, (1, 4)))
+    stage(far_side, (2, 5), (right, (3, 4)))
+    square(across, (0, 3))
     arrive(3)
-    stage(sides, (3, 0), (across, (2, 5)))
-    square(left, (2, 3))
+    stage(sides, (3, 0), (across, (1, 4)))
+    square(across, (2, 5))
     arrive(4)
-    stage(sides, (4, 1), (right, (5, 0)))
+    stage(sides, (4, 1), (left, (2, 3)))
     arrive(5)
-    stage(sides, (5, 2), (left, (4, 5)))
+    stage(sides, (5, 2), (right, (5, 0)))
+    square(left, (4, 5))
     square(right, (1, 2))
 
     for u in (0, 3, 1, 4, 2, 5):

time: 156 us -> 152 us (0.974)
  Pallas kernels: 152 us -> 149 us
    pallas_call x1, Pallas kernels: 152 us -> 149 us  [body(): pl.pallas_call(kernel, out_shape=(block, block), in_specs=[pl.BlockSpec(m...]
where the time goes in v6:
time: 152 us
  Pallas kernels  149 us (98%)
  local copies, waits for them, and re-layouts  2.81 us (2%)
    pallas_call x1, Pallas kernels, body(): pl.pallas_call(kernel, out_shape=(block, block), in_specs=[pl.BlockSpec(m...  149 us

profile of v6, /device:TPU:1, one launch (start us, length us, event | category | flops | bytes accessed | tf_op | source)
XLA Modules:
  0.0 152.0 jit_solution(2871728918533831589)
XLA Ops:
  0.6 148.6 %shard_map.41 = (f32[768,768]{1,0:T(8,128)S(1)}, f32[768,768]{1,0:T(8,128)S(1)}) custom-call(f32[768,768]{1,0:T(8,128)} %a_hbm.1, f32[768,768]{1,0:T(8,128)} %x_hbm.1), custom_call_target="tpu_custom_call" | custom-call | flops 32614907904 | bytes 9437184 | tf_op jit(solution)/shard_map/pallas_call | solution.py:517
  149.2 1.4 copy.6
  150.6 1.4 copy.7

commit v7 on v6

--- a/solution.py
+++ b/solution.py
@@ -97,27 +97,29 @@
     fwd, bwd = (y + sign + 4) % 4, (y - sign + 4) % 4
     before, after, across = (place + 3) % 4, (place + 1) % 4, (place + 2) % 4
 
-    def ring(d, kind, g, slot, half):
-        r0, size = (g * G, G) if half is None else (g * G + half * H, H)
-        part = xcol.at[slot, pl.ds(r0, size), pl.ds(0, (g + 1) * G if slot == 0 else N)]
-        return remote(part, part, rs.at[d, kind, g], rr.at[d, kind, g], {"row": fwd if d == 0 else bwd})
+    def ring(d, kind, slot, u, n=2):
+        part = xcol.at[slot, pl.ds(u * H, n * H), pl.ds(0, (u + n) * H if slot == 0 else N)]
+        return remote(part, part, rs.at[d, kind, u], rr.at[d, kind, u], {"row": fwd if d == 0 else bwd})
 
     def near_of(p, g):
-        go = []
-        if p != 3 or g > 0:
-            go.append((0, 0, g, p, None))
-        if p != 1:
-            go.append((1, 0, g, p, None))
-        return go
+        u = 2 * g
+        if p == 0:
+            return [(d, 0, 0, v, 1) for v in (u, u + 1) for d in range(2)]
+        if p == 1:
+            return [(0, 0, 1, u, 2)]
+        if p == 2:
+            return [(d, 0, 2, u, 2) for d in range(2)]
+        return [(1, 0, 3, u, 2)] + ([], [(0, 0, 3, 3, 1)], [(0, 0, 3, 4, 2)])[g]
 
     def far_of(p, g):
+        u = 2 * g
         if p == 0:
-            return ((), ((0, 1, g, 3, 0),), ((0, 1, g, 3, None),))[g]
+            return ([], [(0, 1, 3, 3, 1)], [(0, 1, 3, 4, 2)])[g]
         if p == 1:
-            return ((0, 1, g, 0, 0 if g == 2 else None), (1, 1, g, 2, None))
+            return [(0, 1, 0, v, 1) for v in (u, u + 1) if v != 2] + [(1, 1, 2, u, 2)]
         if p == 2:
-            return (((1, 1, g, 3, None),), ((1, 1, g, 3, 1),), ())[g]
-        return ((1, 1, g, 0, 1),) if g == 2 else ()
+            return ([(1, 1, 3, 0, 2)], [(1, 1, 3, 2, 1)], [])[g]
+        return [(1, 1, 0, 2, 1)] if g == 1 else []
 
     def into(table, p, g):
         return [t for t in table((p + 3) % 4, g) if t[0] == 0] + [
@@ -160,7 +162,7 @@
         return remote(xcol.at[1, rows], xcol.at[1, rows], ms.at[g], mr.at[g], {"col": partner})
 
     def corner():
-        return remote(xcol.at[3, :, pl.ds(0, G)], zx, cs.at[0], cr.at[0], {"col": other_partner})
+        return remote(xcol.at[3, :, pl.ds(0, NG * H)], zx, cs.at[0], cr.at[0], {"col": other_partner})
 
     def x_near(act, g):
         each_place(lambda p: [act(ring(*t)) for t in near_of(p, g)])
@@ -189,10 +191,9 @@
         each_place(land)
 
     def mirror():
-        for g, h in ((0, 1), (0, 2), (1, 2)):
-            xcol[0, g * G : (g + 1) * G, h * G : (h + 1) * G] = xcol[
-                0, h * G : (h + 1) * G, g * G : (g + 1) * G
-            ].T
+        for u in range(NU - 1):
+            v = slice((u + 1) * H, N)
+            xcol[0, u * H : (u + 1) * H, v] = xcol[0, v, u * H : (u + 1) * H].T
 
     def begin(copy):
         copy.start()
@@ -230,10 +231,6 @@
     row_partner.start()
 
     a_begin(0, (0, 1, 2), (0,))
-
-    @pl.when(place == 3)
-    def _():
-        corner().start()
 
 
     def convert(ref, r0, j):
@@ -329,6 +326,11 @@
         x_near_in(2)
     x_far(begin, 2)
 
+
+    @pl.when(place == 3)
+    def _():
+        corner().start()
+
     a_begin(0, (1, 2), (1, 2))
     a_begin(1, (0, 1, 2), (1,))
     a_begin(1, (1, 2), (2, 3))
@@ -345,10 +347,7 @@
     def _(g):
         y_step(place, g)
 
-    @pl.loop(1, NG)
-    def _(g):
-        y_near(g)
-
+    y_near(2)
     with jax.named_scope("xfar"):
         for g in range(NG):
             x_far_in(g)
@@ -357,18 +356,22 @@
         def _():
             mirror()
 
+    @pl.loop(0, NG)
+    def _(g):
+        y_step(across, g)
+
+    arrive(0)
+    start(a_out(6))
+    with jax.named_scope("corner"):
+
         @pl.when(place == 0)
         def _():
             corner().wait_recv()
-            xcol[3, :G, :] = zx[...].T
-
-    y_near(0)
-    arrive(0)
-    start(a_out(6))
-
-    @pl.loop(0, NG)
+            xcol[3, : NG * H, :] = zx[...].T
+
+    @pl.loop(0, 2)
     def _(g):
-        y_step(across, g)
+        y_near(g)
 
     @pl.loop(0, NG)
     def _(m):
@@ -532,10 +535,10 @@
                 pltpu.VMEM((4, NU, N, H), F32),
                 pltpu.VMEM((2, NU, N, H), F32),
                 pltpu.VMEM((NU, N, H), F32),
-                pltpu.VMEM((N, G), F32),
+                pltpu.VMEM((N, NG * H), F32),
                 dma((2,)),
-                dma((2, 2, NG)),
-                dma((2, 2, NG)),
+                dma((2, 2, NU)),
+                dma((2, 2, NU)),
                 dma((2, 9)),
                 dma((2, 9)),
                 dma((NG,)),

time: 152 us -> 150 us (0.987)
  Pallas kernels: 149 us -> 147 us
    pallas_call x1, Pallas kernels: 149 us -> 147 us  [body(): pl.pallas_call(kernel, out_shape=(block, block), in_specs=[pl.BlockSpec(m...]
where the time goes in v7:
time: 150 us
  Pallas kernels  147 us (98%)
  local copies, waits for them, and re-layouts  2.81 us (2%)
    pallas_call x1, Pallas kernels, body(): pl.pallas_call(kernel, out_shape=(block, block), in_specs=[pl.BlockSpec(m...  147 us

profile of v7, /device:TPU:1, one launch (start us, length us, event | category | flops | bytes accessed | tf_op | source)
XLA Modules:
  0.0 150.2 jit_solution(4294757194630561572)
XLA Ops:
  0.6 146.7 %shard_map.41 = (f32[768,768]{1,0:T(8,128)S(1)}, f32[768,768]{1,0:T(8,128)S(1)}) custom-call(f32[768,768]{1,0:T(8,128)} %a_hbm.1, f32[768,768]{1,0:T(8,128)} %x_hbm.1), custom_call_target="tpu_custom_call" | custom-call | flops 32614907904 | bytes 9437184 | tf_op jit(solution)/shard_map/pallas_call | solution.py:520
  147.3 1.4 copy.6
  148.8 1.4 copy.7

commit v8 on v7

--- a/solution.py
+++ b/solution.py
@@ -65,6 +65,8 @@
     pr,
     zs,
     zr,
+    hs,
+    hr,
 ):
     y = lax.axis_index("row")
     c = lax.axis_index("col")
@@ -104,7 +106,7 @@
     def near_of(p, g):
         u = 2 * g
         if p == 0:
-            return [(d, 0, 0, v, 1) for v in (u, u + 1) for d in range(2)]
+            return [(d, 0, 0, v, 1) for v in ((0, 1), (2, 3, 4, 5), ())[g] for d in range(2)]
         if p == 1:
             return [(0, 0, 1, u, 2)]
         if p == 2:
@@ -116,7 +118,7 @@
         if p == 0:
             return ([], [(0, 1, 3, 3, 1)], [(0, 1, 3, 4, 2)])[g]
         if p == 1:
-            return [(0, 1, 0, v, 1) for v in (u, u + 1) if v != 2] + [(1, 1, 2, u, 2)]
+            return [(0, 1, 0, v, 1) for v in ((0, 1), (3, 4, 5), ())[g]] + [(1, 1, 2, u, 2)]
         if p == 2:
             return ([(1, 1, 3, 0, 2)], [(1, 1, 3, 2, 1)], [])[g]
         return [(1, 1, 0, 2, 1)] if g == 1 else []
@@ -332,12 +334,12 @@
         corner().start()
 
     a_begin(0, (1, 2), (1, 2))
-    a_begin(1, (0, 1, 2), (1,))
     a_begin(1, (1, 2), (2, 3))
     a_begin(1, (0,), (0,))
     row_in(2)
     a_begin(0, (0, 1, 2), (3,))
     a_begin(1, (1, 2), (0,))
+    a_begin(1, (0, 1, 2), (1,))
 
     @pl.when(place % 2 == 1)
     def _():
@@ -423,6 +425,50 @@
                 @pl.when(q == 1)
                 def _():
                     to_other(u[k]).start()
+
+    odd = (y + c) % 2 == 1
+    from_left = role(left)[0] == 1
+    last_s = jnp.where(from_left, left, right), jnp.where(from_left, right, left)
+    last_u = jnp.where(from_left, 5, 2), jnp.where(from_left, 2, 5)
+
+    def half_to_partner(k, h):
+        q, rows = 1 - k, pl.ds(h * (N // 2), N // 2)
+        return remote(
+            part.at[q, last_u[k], rows],
+            precv.at[q, last_u[k], rows],
+            hs.at[k, h],
+            hr.at[k, h],
+            {"col": partner},
+        )
+
+    def half_to_other(u, h):
+        rows = pl.ds(h * (N // 2), N // 2)
+        return remote(part.at[3, u, rows], pzrecv.at[u, rows], hs.at[2, h], hr.at[2, h], {"col": other})
+
+    def last_sums():
+        for k in range(2):
+            split_unit(acol, last_s[k], last_u[k], k)
+        for h in range(2):
+            rows = slice(h * (N // 2), (h + 1) * (N // 2))
+            value = dot3(yh[rows, :], yl[rows, :], ch[...], cl[...], NT)
+            for k in range(2):
+                part[1 - k + 2 * odd.astype(jnp.int32), last_u[k], rows] = value[:, k * H : (k + 1) * H]
+
+            @pl.when(jnp.logical_not(odd))
+            def _():
+                for k in range(2):
+                    half_to_partner(k, h).start()
+
+    def last_collect(k):
+        @pl.when(odd)
+        def _():
+            for h in range(2):
+                rows = slice(h * (N // 2), (h + 1) * (N // 2))
+                with jax.named_scope("pwait"):
+                    half_to_partner(k, h).wait_recv()
+                part[3 - k, last_u[k], rows] += precv[1 - k, last_u[k], rows]
+                if k == 0:
+                    half_to_other(last_u[0], h).start()
 
     def square(s, u):
         with jax.named_scope("a2"):
@@ -473,13 +519,27 @@
     arrive(4)
     stage(sides, (4, 1), (left, (2, 3)))
     arrive(5)
-    stage(sides, (5, 2), (right, (5, 0)))
+    with jax.named_scope("p"):
+        last_sums()
+    last_collect(0)
+    square(right, (5, 0))
+    last_collect(1)
     square(left, (4, 5))
     square(right, (1, 2))
 
     for u in (0, 3, 1, 4, 2, 5):
+        halves = jnp.logical_and(odd, u == jnp.where((y - c + 4) % 4 == 1, 5, 2))
         with jax.named_scope("z"):
-            to_other(u).wait_recv()
+
+            @pl.when(jnp.logical_not(halves))
+            def _():
+                to_other(u).wait_recv()
+
+            @pl.when(halves)
+            def _():
+                for h in range(2):
+                    half_to_other(u, h).wait_recv()
+
         lanes = slice(u * H, (u + 1) * H)
         xo[:, lanes] = xcol[place, :, lanes] + (part[2, u] + pzrecv[u])
 
@@ -497,9 +557,26 @@
             copy.wait_send()
 
     for u in range(NU):
-        to_partner(0, u).wait_send()
-        to_partner(1, u).wait_send()
-        to_other(u).wait_send()
+        for k in range(2):
+
+            @pl.when(jnp.logical_or(odd, u != last_u[k]))
+            def _():
+                to_partner(1 - k, u).wait_send()
+
+        @pl.when(jnp.logical_or(jnp.logical_not(odd), u != last_u[0]))
+        def _():
+            to_other(u).wait_send()
+
+    for h in range(2):
+
+        @pl.when(odd)
+        def _():
+            half_to_other(last_u[0], h).wait_send()
+
+        @pl.when(jnp.logical_not(odd))
+        def _():
+            for k in range(2):
+                half_to_partner(k, h).wait_send()
 
     @pl.when(jnp.logical_or(place == 1, place == 2))
     def _():
@@ -511,6 +588,17 @@
         corner().wait_send()
 
     row_partner.wait_send()
+
+
+def flush(xo, a2, xo_hbm, a2_hbm, sem):
+    copies = [
+        pltpu.make_async_copy(src, dst, sem.at[i])
+        for i, (src, dst) in enumerate(((xo, xo_hbm), (a2, a2_hbm)))
+    ]
+    for copy in copies:
+        copy.start()
+    for copy in copies:
+        copy.wait()
 
 
 def solution(mesh):
@@ -551,13 +639,24 @@
                 dma((2, NU)),
                 dma((NU,)),
                 dma((NU,)),
+                dma((3, 2)),
+                dma((3, 2)),
             ],
             compiler_params=pltpu.CompilerParams(
                 collective_id=0, has_side_effects=True, vmem_limit_bytes=57 * 2**20
             ),
             cost_estimate=pl.CostEstimate(flops=32614907904, bytes_accessed=9437184, transcendentals=0),
         )(a, x)
-        return xo, a2
+        out = jax.ShapeDtypeStruct((N, N), F32)
+        return pl.pallas_call(
+            flush,
+            out_shape=(out, out),
+            in_specs=[pl.BlockSpec(memory_space=pltpu.VMEM)] * 2,
+            out_specs=[pl.BlockSpec(memory_space=pl.ANY)] * 2,
+            scratch_shapes=[dma((2,))],
+            compiler_params=pltpu.CompilerParams(vmem_limit_bytes=2**20),
+            cost_estimate=pl.CostEstimate(flops=0, bytes_accessed=9437184, transcendentals=0),
+        )(xo, a2)
 
     spec = P(("eq", "row"), "col")
     return jax.shard_map(

time: 150 us -> 150 us (level)
  local copies, waits for them, and re-layouts: 2.81 us -> 0 us
  Pallas kernels: 147 us -> 149 us
    unnamed x2 -> x0, local copies, waits for them, and re-layouts: 2.81 us -> none
    pallas_call x0 -> x1, Pallas kernels: none -> 2.2 us  [body(): pl.pallas_call(flush, out_shape=(out, out), in_specs=[pl.BlockSpec(memory...]
where the time goes in v8:
time: 150 us
  Pallas kernels  149 us (99%)
    pallas_call x1, Pallas kernels, body(): pl.pallas_call(kernel, out_shape=(block, block), in_specs=[pl.BlockSpec(m...  147 us

profile of v8, /device:TPU:1, one launch (start us, length us, event | category | flops | bytes accessed | tf_op | source)
XLA Modules:
  0.0 149.8 jit_solution(7857223865639293020)
XLA Ops:
  0.6 146.8 %shard_map.41 = (f32[768,768]{1,0:T(8,128)S(1)}, f32[768,768]{1,0:T(8,128)S(1)}) custom-call(f32[768,768]{1,0:T(8,128)} %a_hbm.1, f32[768,768]{1,0:T(8,128)} %x_hbm.1), custom_call_target="tpu_custom_call" | custom-call | flops 32614907904 | bytes 9437184 | tf_op jit(solution)/shard_map/pallas_call | solution.py:608
  147.5 2.2 %shard_map.42 = (f32[768,768]{1,0:T(8,128)}, f32[768,768]{1,0:T(8,128)}) custom-call(f32[768,768]{1,0:T(8,128)S(1)} %get-tuple-element.4.xo, f32[768,768]{1,0:T(8,128)S(1)} %get-tuple-element.5.a2), custom_call_target="tpu_custom_call" | custom-call | bytes 9437184 | tf_op jit(solution)/shard_map/pallas_call | solution.py:651

commit v9 on v8

--- a/solution.py
+++ b/solution.py
@@ -431,6 +431,9 @@
     last_s = jnp.where(from_left, left, right), jnp.where(from_left, right, left)
     last_u = jnp.where(from_left, 5, 2), jnp.where(from_left, 2, 5)
 
+    def crossing(u, v):
+        return jnp.where(from_left, u, v), jnp.where(from_left, v, u)
+
     def half_to_partner(k, h):
         q, rows = 1 - k, pl.ds(h * (N // 2), N // 2)
         return remote(
@@ -448,15 +451,14 @@
     def last_sums():
         for k in range(2):
             split_unit(acol, last_s[k], last_u[k], k)
-        for h in range(2):
-            rows = slice(h * (N // 2), (h + 1) * (N // 2))
-            value = dot3(yh[rows, :], yl[rows, :], ch[...], cl[...], NT)
+        value = dot3(yh[...], yl[...], ch[...], cl[...], NT)
+        for k in range(2):
+            part[1 - k + 2 * odd.astype(jnp.int32), last_u[k]] = value[:, k * H : (k + 1) * H]
+
+        @pl.when(jnp.logical_not(odd))
+        def _():
             for k in range(2):
-                part[1 - k + 2 * odd.astype(jnp.int32), last_u[k], rows] = value[:, k * H : (k + 1) * H]
-
-            @pl.when(jnp.logical_not(odd))
-            def _():
-                for k in range(2):
+                for h in range(2):
                     half_to_partner(k, h).start()
 
     def last_collect(k):
@@ -484,19 +486,19 @@
         square(*meanwhile)
         collect(s, u)
 
-    own, sides, far_side = (place, place), (left, right), (across, across)
+    own, far_side = (place, place), (across, across)
     arrive(1)
     start(a_out(7))
-    sums(sides, (0, 3))
-    sums(sides, (1, 4))
-    collect(sides, (0, 3))
+    sums(last_s, crossing(0, 3))
+    sums(last_s, crossing(1, 4))
+    collect(last_s, crossing(0, 3))
     arrive(2)
     for i in (8, 3, 4, 5):
         start(a_out(i))
-    sums(sides, (2, 5))
-    collect(sides, (1, 4))
+    sums(last_s, crossing(2, 5))
+    collect(last_s, crossing(1, 4))
     sums(own, (0, 3))
-    collect(sides, (2, 5))
+    collect(last_s, crossing(2, 5))
     sums(own, (1, 4))
     collect(own, (0, 3))
     sums(own, (2, 5))
@@ -514,10 +516,10 @@
     stage(far_side, (2, 5), (right, (3, 4)))
     square(across, (0, 3))
     arrive(3)
-    stage(sides, (3, 0), (across, (1, 4)))
+    stage(last_s, crossing(3, 0), (across, (1, 4)))
     square(across, (2, 5))
     arrive(4)
-    stage(sides, (4, 1), (left, (2, 3)))
+    stage(last_s, crossing(4, 1), (left, (2, 3)))
     arrive(5)
     with jax.named_scope("p"):
         last_sums()

time: 150 us -> 149 us (level)
  no operation moved by 1% of the time
where the time goes in v9:
time: 149 us
  Pallas kernels  148 us (99%)
    pallas_call x1, Pallas kernels, body(): pl.pallas_call(kernel, out_shape=(block, block), in_specs=[pl.BlockSpec(m...  146 us

profile of v9, /device:TPU:1, one launch (start us, length us, event | category | flops | bytes accessed | tf_op | source)
XLA Modules:
  0.0 149.3 jit_solution(8135519645694436268)
XLA Ops:
  0.6 146.3 %shard_map.41 = (f32[768,768]{1,0:T(8,128)S(1)}, f32[768,768]{1,0:T(8,128)S(1)}) custom-call(f32[768,768]{1,0:T(8,128)} %a_hbm.1, f32[768,768]{1,0:T(8,128)} %x_hbm.1), custom_call_target="tpu_custom_call" | custom-call | flops 32614907904 | bytes 9437184 | tf_op jit(solution)/shard_map/pallas_call | solution.py:610
  146.9 2.2 %shard_map.42 = (f32[768,768]{1,0:T(8,128)}, f32[768,768]{1,0:T(8,128)}) custom-call(f32[768,768]{1,0:T(8,128)S(1)} %get-tuple-element.4.xo, f32[768,768]{1,0:T(8,128)S(1)} %get-tuple-element.5.a2), custom_call_target="tpu_custom_call" | custom-call | bytes 9437184 | tf_op jit(solution)/shard_map/pallas_call | solution.py:653

commit v10 on v9

--- a/solution.py
+++ b/solution.py
@@ -288,7 +288,7 @@
 
             @pl.when(flipped)
             def _():
-                @pl.loop(0, NG)
+                @pl.loop(0, NG, unroll=True)
                 def _(k):
                     v = (2 * k, 2 * k + 1)
                     lanes = lanes_of(k)

time: 149 us -> 149 us (level)
  no operation moved by 1% of the time
where the time goes in v10:
time: 149 us
  Pallas kernels  148 us (99%)
    pallas_call x1, Pallas kernels, body(): pl.pallas_call(kernel, out_shape=(block, block), in_specs=[pl.BlockSpec(m...  146 us

profile of v10, /device:TPU:1, one launch (start us, length us, event | category | flops | bytes accessed | tf_op | source)
XLA Modules:
  0.0 149.3 jit_solution(7474344023450998930)
XLA Ops:
  0.6 146.3 %shard_map.41 = (f32[768,768]{1,0:T(8,128)S(1)}, f32[768,768]{1,0:T(8,128)S(1)}) custom-call(f32[768,768]{1,0:T(8,128)} %a_hbm.1, f32[768,768]{1,0:T(8,128)} %x_hbm.1), custom_call_target="tpu_custom_call" | custom-call | flops 32614907904 | bytes 9437184 | tf_op jit(solution)/shard_map/pallas_call | solution.py:610
  146.9 2.2 %shard_map.42 = (f32[768,768]{1,0:T(8,128)}, f32[768,768]{1,0:T(8,128)}) custom-call(f32[768,768]{1,0:T(8,128)S(1)} %get-tuple-element.4.xo, f32[768,768]{1,0:T(8,128)S(1)} %get-tuple-element.5.a2), custom_call_target="tpu_custom_call" | custom-call | bytes 9437184 | tf_op jit(solution)/shard_map/pallas_call | solution.py:653
